TPU v7x, 256 devices: a whole 4x4x8 slice. The times are simulated.
256 devices in a mesh: row: 32 (over x, y, core), col: 8 (over z).
Axes of the slice: x: 4, y: 4, z: 8, core: 2. Of those that a mesh axis runs over, the one named last changes fastest.
Arguments:
- hidden: bfloat16 [64, 6144], P('col', 'row'), may hold values from -6 to 6
- queries: bfloat16 [64, 6144], P('row', 'col'), may hold values from -48 to 48
- new_keys: bfloat16 [64, 1024], P('row', 'col'), may hold values from -4 to 4
- new_values: bfloat16 [64, 1024], P('row', 'col'), may hold values from -6 to 6
- cache_keys: bfloat16 [64, 2048, 1024], P('row', None, 'col'), may hold values from -6 to 6
- cache_values: bfloat16 [64, 2048, 1024], P('row', None, 'col'), may hold values from -6 to 6
- lengths: int32 [64], P('row'), may hold values from 1 to 2048, 65536 in all
- page_table: int32 [64, 8], replicated, may hold values from 0 to 63
- resident: int32 [32, 4], replicated, may hold values from 0 to 63, as said below
- prefix_keys: bfloat16 [32, 4, 128, 1024], P('row', None, None, 'col'), may hold values from -4 to 4, as said below
- prefix_values: bfloat16 [32, 4, 128, 1024], P('row', None, None, 'col'), may hold values from -16 to 16, as said below
- out_weight: bfloat16 [6144, 6144], P('col', 'row'), may hold values from -0.078125 to 0.078125
- norm_gain: float32 [6144], P('row'), may hold values from 0.5 to 1.5
- router_weight: bfloat16 [6144, 8], P('row'), may hold values from -0.078125 to 0.078125
- experts: int32 [64, 2], P('col'), may hold values from 0 to 7, all different within a row; in each aligned block of 8 rows (0 to 7, 8 to 15, ...) at most 4 rows name the same one
- gate_weight: bfloat16 [8, 6144, 8192], P('col', None, 'row'), may hold values from -0.078125 to 0.078125
- up_weight: bfloat16 [8, 6144, 8192], P('col', None, 'row'), may hold values from -0.078125 to 0.078125
- down_projection_weight: bfloat16 [8, 8192, 6144], P('col', 'row'), may hold values from -0.0625 to 0.0625
Outputs:
- layer_out: bfloat16 [64, 6144], P('col', 'row')
Inputs may be any that keep to these rules, and one draw needn't show every extreme that they name: `resident`: each row's 4 slots hold different page ids, and every id below 64 is held by at least one row. `prefix_keys`: slots holding the same page id hold the same keys, on every row. `prefix_values`: slots holding the same page id hold the same values, on every row. The two experts of a token differ; in each aligned block of 8 tokens at most 4 tokens name the same expert.
All inputs are finite; a program needn't handle non-finite values. No bound on the sum of `lengths` on one device may be relied on, other than what follows from the above.
Results may differ from a plain program's by a relative error of at most 0.0095.
Values may be sent and summed in bfloat16 or wider, within the bound.
A program may use at most 128 MiB of HBM per device.

v0:
```python
import math

import jax
import jax.numpy as jnp
from jax import lax
from jax.sharding import PartitionSpec as P

D = 6144
HQ = 48
KVH = 8
HD = 128
EXPERT_COUNT = 8
EXPERTS_PER_TOKEN = 2
PRE_HOME = 2


NEG = -1e30
EPS = 1e-05


def in_one_piece(arrays, axis, dim, along):
    both = jnp.concatenate(arrays, axis=along)
    filled, at, done = (lax.all_gather(both, axis, axis=dim, tiled=True), 0, [])
    for a in arrays:
        done.append(lax.slice_in_dim(filled, at, at + a.shape[along], axis=along))
        at += a.shape[along]
    return tuple(done)


def sent_to_all(value, axis):
    size = lax.axis_size(axis)
    return lax.all_to_all(
        jnp.broadcast_to(value[None], (size, *value.shape)), axis, 0, 0, tiled=True
    )


def joined_along(parts, dim):
    dims = list(parts.shape[1:])
    dims[dim] *= parts.shape[0]
    return jnp.moveaxis(parts, 0, dim).reshape(dims)


def gathered_copies(value, axis, dim):
    parts = sent_to_all(value, axis)
    return joined_along(parts, dim)


def split_up(value, dim, size):
    dims = value.shape
    parts = value.reshape(*dims[:dim], size, dims[dim] // size, *dims[dim + 1 :])
    return jnp.moveaxis(parts, dim, 0)


def summed_on_arrival(value, axis, dim):
    parts = split_up(value, dim, lax.axis_size(axis))
    arrived = lax.all_to_all(parts, axis, split_axis=0, concat_axis=0, tiled=True)
    return arrived.astype(jnp.float32).sum(axis=0)


def taken_together(value, axis):
    everything = sent_to_all(value, axis)
    return jnp.sum(everything, axis=0)


def holder_table(resident, npages):
    flat = resident.reshape(-1)
    count = flat.shape[0]
    places = jnp.arange(count, dtype=jnp.int32)
    hits = flat[None, :] == jnp.arange(npages, dtype=jnp.int32)[:, None]
    return jnp.min(jnp.where(hits, places[None, :], count), axis=1)


def lookup(table, wanted, npages):
    match = wanted[..., None] == jnp.arange(npages, dtype=jnp.int32)
    return jnp.sum(jnp.where(match, table, 0), axis=-1)


def body(
    hidden,
    queries,
    new_keys,
    new_values,
    cache_keys,
    cache_values,
    lengths,
    page_table,
    resident,
    prefix_keys,
    prefix_values,
    out_weight,
    norm_gain,
    router_weight,
    experts,
    gate_weight,
    up_weight,
    down_projection_weight,
):
    seq_row = queries.shape[0]
    kv_local = new_keys.shape[1] // HD
    group = HQ // KVH
    scale = 1.0 / math.sqrt(HD)
    row_count = lax.axis_size("row")
    col_count = lax.axis_size("col")
    row_here = lax.axis_index("row")
    slots = resident.shape[1]
    npages = PRE_HOME * row_count
    holder = holder_table(resident, npages)
    context = cache_keys.shape[1]
    own_start = row_here * seq_row
    query = queries.reshape(seq_row, kv_local, group, HD)
    keys_own = cache_keys.reshape(seq_row, context, kv_local, HD)
    values_own = cache_values.reshape(seq_row, context, kv_local, HD)
    fresh_keys = new_keys.reshape(seq_row, kv_local, HD)
    fresh_values = new_values.reshape(seq_row, kv_local, HD)
    live = jnp.arange(context, dtype=jnp.int32)[None, :] < lengths[:, None]
    own_scores = (
        jnp.einsum("skgd,stkd->skgt", query, keys_own, preferred_element_type=jnp.float32) * scale
    )
    own_scores = jnp.where(live[:, None, None, :], own_scores, NEG)
    fresh_scores = (
        jnp.einsum("skgd,skd->skg", query, fresh_keys, preferred_element_type=jnp.float32) * scale
    )
    own_peak = jnp.maximum(jnp.max(own_scores, axis=-1), fresh_scores)
    pool_keys, pool_values = in_one_piece((prefix_keys, prefix_values), "row", 0, 1)
    page = pool_keys.shape[2]
    pool_keys = pool_keys.reshape(row_count * slots, page, kv_local * HD)
    pool_values = pool_values.reshape(row_count * slots, page, kv_local * HD)
    own_tables = lax.dynamic_slice_in_dim(page_table, own_start, seq_row, 0)
    places = lookup(holder, own_tables, npages).reshape(-1)
    pre_keys = jnp.take(pool_keys, places, axis=0).reshape(seq_row, -1, kv_local, HD)
    pre_values = jnp.take(pool_values, places, axis=0).reshape(seq_row, -1, kv_local, HD)
    pre_scores = (
        jnp.einsum("skgd,stkd->skgt", query, pre_keys, preferred_element_type=jnp.float32) * scale
    )
    peak = jnp.maximum(own_peak, jnp.max(pre_scores, axis=-1))
    pre_expo = jnp.exp(pre_scores - peak[..., None])
    summed = jnp.einsum(
        "skgt,stkd->skgd",
        pre_expo.astype(jnp.bfloat16),
        pre_values,
        preferred_element_type=jnp.float32,
    )
    total = jnp.sum(pre_expo, axis=-1)
    own_expo = jnp.exp(own_scores - peak[..., None])
    fresh_expo = jnp.exp(fresh_scores - peak)
    summed = summed + jnp.einsum(
        "skgt,stkd->skgd",
        own_expo.astype(jnp.bfloat16),
        values_own,
        preferred_element_type=jnp.float32,
    )
    summed = summed + jnp.einsum(
        "skg,skd->skgd",
        fresh_expo.astype(jnp.bfloat16),
        fresh_values,
        preferred_element_type=jnp.float32,
    )
    total = total + jnp.sum(own_expo, axis=-1) + fresh_expo
    attended = (
        (summed / total[..., None]).reshape(seq_row, kv_local * group * HD).astype(jnp.bfloat16)
    )
    projected = jnp.dot(
        gathered_copies(attended, "row", 0), out_weight, preferred_element_type=jnp.float32
    )
    projected = summed_on_arrival(projected.astype(jnp.bfloat16), "col", 0)
    residual = hidden.astype(jnp.float32) + projected
    squares = taken_together(jnp.sum(residual * residual, axis=1), "row")
    inverse = lax.rsqrt(squares / D + EPS)
    normed = (residual * inverse[:, None] * norm_gain[None, :]).astype(jnp.bfloat16)
    logits = taken_together(
        jnp.dot(normed, router_weight, preferred_element_type=jnp.float32), "row"
    )
    token_rows = experts.shape[0]
    hidden_width = hidden.shape[1]
    chosen_hot = experts[:, :, None] == jnp.arange(EXPERT_COUNT, dtype=jnp.int32)[None, None, :]
    chosen = jnp.sum(jnp.where(chosen_hot, logits[:, None, :], 0.0), axis=2)
    first = 1.0 / (1.0 + jnp.exp(chosen[:, 1] - chosen[:, 0]))
    second = 1.0 / (1.0 + jnp.exp(chosen[:, 0] - chosen[:, 1]))
    gates = jnp.stack([first, second], axis=1)
    flat_hot = chosen_hot.reshape(token_rows * EXPERTS_PER_TOKEN, EXPERT_COUNT).astype(jnp.int32)
    ranks = jnp.sum((jnp.cumsum(flat_hot, axis=0) - flat_hot) * flat_hot, axis=1)
    per_col = EXPERT_COUNT // col_count
    expert_capacity = 2 * token_rows * EXPERTS_PER_TOKEN // EXPERT_COUNT
    flat_ids = experts.reshape(-1)
    slot_position = (flat_ids % per_col * col_count + flat_ids // per_col) * expert_capacity + ranks
    slot_number = EXPERT_COUNT * expert_capacity
    expert_picks = (
        slot_position[:, None] == jnp.arange(slot_number, dtype=jnp.int32)[None, :]
    ).reshape(token_rows, EXPERTS_PER_TOKEN, slot_number)
    dispatch = jnp.sum(expert_picks.astype(jnp.float32), axis=1).astype(jnp.bfloat16)
    combine = jnp.sum(jnp.where(expert_picks, gates[:, :, None], 0.0), axis=1)
    rows_in = col_count * expert_capacity
    outgoing = lax.dot_general(
        dispatch, normed, (((0,), (0,)), ((), ())), preferred_element_type=jnp.float32
    ).astype(jnp.bfloat16)
    outgoing = outgoing.reshape(per_col, col_count, expert_capacity, hidden_width)
    incoming = lax.all_to_all(outgoing, "col", split_axis=1, concat_axis=1, tiled=True).reshape(
        per_col, rows_in, hidden_width
    )
    piece = gathered_copies(incoming, "row", 2)
    inner_gate = jnp.einsum("emd,edf->emf", piece, gate_weight, preferred_element_type=jnp.float32)
    inner_up = jnp.einsum("emd,edf->emf", piece, up_weight, preferred_element_type=jnp.float32)
    activated_hidden = (jax.nn.silu(inner_gate) * inner_up).astype(jnp.bfloat16)
    expert_term = jnp.einsum(
        "rsw,rwp->prs", activated_hidden, down_projection_weight, preferred_element_type=jnp.float32
    )
    outputs = summed_on_arrival(
        expert_term.reshape(hidden_width * lax.axis_size("row"), per_col * rows_in).astype(
            jnp.bfloat16
        ),
        "row",
        0,
    )
    outputs = outputs.astype(jnp.bfloat16).reshape(
        hidden_width, per_col, col_count, expert_capacity
    )
    returned = lax.all_to_all(outputs, "col", split_axis=2, concat_axis=2, tiled=True).reshape(
        hidden_width, slot_number
    )
    mixed = lax.dot_general(combine, returned.astype(jnp.float32), (((1,), (1,)), ((), ())))
    return (residual + mixed).astype(jnp.bfloat16)


def solution(mesh):
    in_specs = (
        P("col", "row"),
        P("row", "col"),
        P("row", "col"),
        P("row", "col"),
        P("row", None, "col"),
        P("row", None, "col"),
        P("row"),
        P(),
        P(),
        P("row", None, None, "col"),
        P("row", None, None, "col"),
        P("col", "row"),
        P("row"),
        P("row", None),
        P("col", None),
        P("col", None, "row"),
        P("col", None, "row"),
        P("col", "row", None),
    )
    out_specs = P("col", "row")
    return jax.shard_map(body, mesh=mesh, in_specs=in_specs, out_specs=out_specs, check_vma=False)
```

profile of v0, /device:TPU:1, one launch (start us, length us, event | category | flops | bytes accessed | tf_op | source)
XLA Modules:
  0.0 215.9 jit_solution(3761852071337690915)
XLA Ops:
  6.5 1.8 pad_maximum_fusion
  8.4 0.8 copy.49
  9.3 0.8 constant_dynamic-slice_fusion
  10.3 0.2 select_reduce_fusion.4
  10.6 0.7 reshape.219
  11.3 0.7 convert.8
  11.9 0.8 fusion.39
  12.7 0.7 iota_compare_fusion.1
  13.5 1.7 fusion.44
  15.1 56.8 %all-gather.2.cloned.1.call-done = bf16[32,8,128,128]{3,2,1,0:T(8,128)(2,1)} async-done(((bf16[1,8,128,128]{3,2,1,0:T(8,128)(2,1)}), bf16[32,8,128,128]{3,2,1,0:T(8,128)(2,1)}) %all-gather.2.cloned.1.call-update) | async-done | bytes 8388624 | tf_op jit(solution)/shard_map/all_gather | solution.py:23
  71.9 6.0 %fusion.42 = (bf16[32,4,128,128]{3,2,1,0:T(8,128)(2,1)}, bf16[32,4,128,128]{3,2,1,0:T(8,128)(2,1)}) fusion(bf16[32,8,128,128]{3,2,1,0:T(8,128)(2,1)} %all-gather.2.cloned.1.call-done), kind=kLoop, calls=%fused_computation.78 | loop fusion | bytes 16777216 | tf_op jit(solution)/shard_map/slice | solution.py:25
  78.0 3.6 %gather_fusion = bf16[16,128,128]{2,1,0:T(8,128)(2,1)} fusion(bf16[128,128,128]{2,1,0:T(8,128)(2,1)} %bitcast.64, s32[1024]{0:T(1024)S(1)} %pad_clamp_fusion), kind=kCustom, calls=%fused_computation.clone | custom fusion | bytes 1048640 | tf_op jit(solution)/shard_map/jit(_take)/gather | solution.py:130
  81.5 3.6 %gather_fusion.1 = bf16[16,128,128]{2,1,0:T(8,128)(2,1)} fusion(bf16[128,128,128]{2,1,0:T(8,128)(2,1)} %bitcast.63, s32[1024]{0:T(1024)S(1)} %pad_clamp_fusion), kind=kCustom, calls=%fused_computation.1.clone | custom fusion | bytes 1048640 | tf_op jit(solution)/shard_map/jit(_take)/gather | solution.py:131
  85.2 1.4 broadcast_select_fusion.1
  86.6 0.3 fusion.43
  87.0 0.2 fusion.26
  87.1 0.2 fusion.28
  87.4 0.2 fusion.22
  87.6 0.3 fusion.19
  87.9 0.7 broadcast_in_dim.114
  88.6 5.5 %all-to-all-start = ((bf16[32,2,768]{2,1,0:T(2,128)(2,1)}), bf16[32,2,768]{2,1,0:T(2,128)(2,1)S(1)}, u32[]{:S(2)}, u32[]{:S(2)}) async-start(bf16[32,2,768]{2,1,0:T(2,128)(2,1)} %broadcast_in_dim.114), calls=%async_computation | async-start | bytes 196608 | tf_op jit(solution)/shard_map/all_to_all | solution.py:32
  94.3 7.3 %all-to-all-done = bf16[32,2,768]{2,1,0:T(2,128)(2,1)S(1)} async-done(((bf16[32,2,768]{2,1,0:T(2,128)(2,1)}), bf16[32,2,768]{2,1,0:T(2,128)(2,1)S(1)}, u32[]{:S(2)}, u32[]{:S(2)}) %all-to-all-start) | async-done | bytes 98336 | tf_op jit(solution)/shard_map/all_to_all | solution.py:32
  101.6 1.8 fusion.11
  103.4 6.7 %all-to-all-start.1 = ((bf16[8,8,192]{2,1,0:T(8,128)(2,1)}), bf16[8,8,192]{2,1,0:T(8,128)(2,1)S(1)}, u32[]{:S(2)}, u32[]{:S(2)}) async-start(bf16[8,8,192]{2,1,0:T(8,128)(2,1)} %fusion.11), calls=%async_computation.1 | async-start | bytes 65536 | tf_op jit(solution)/shard_map/all_to_all | solution.py:56
  110.2 6.9 %all-to-all-done.1 = bf16[8,8,192]{2,1,0:T(8,128)(2,1)S(1)} async-done(((bf16[8,8,192]{2,1,0:T(8,128)(2,1)}), bf16[8,8,192]{2,1,0:T(8,128)(2,1)S(1)}, u32[]{:S(2)}, u32[]{:S(2)}) %all-to-all-start.1) | async-done | bytes 24608 | tf_op jit(solution)/shard_map/all_to_all | solution.py:56
  117.1 0.1 multiply_reduce_fusion
  117.2 0.6 broadcast_in_dim.115
  117.9 5.2 %all-to-all-start.2 = ((f32[32,1,8]{2,1,0:T(1,128)}), f32[32,1,8]{2,1,0:T(1,128)S(1)}, u32[]{:S(2)}, u32[]{:S(2)}) async-start(f32[32,1,8]{2,1,0:T(1,128)} %broadcast_in_dim.115), calls=%async_computation.2 | async-start | bytes 32768 | tf_op jit(solution)/shard_map/all_to_all | solution.py:32
  123.1 0.2 select_reduce_fusion.3
  123.4 6.8 %all-to-all-done.2 = f32[32,1,8]{2,1,0:T(1,128)S(1)} async-done(((f32[32,1,8]{2,1,0:T(1,128)}), f32[32,1,8]{2,1,0:T(1,128)S(1)}, u32[]{:S(2)}, u32[]{:S(2)}) %all-to-all-start.2) | async-done | bytes 1056 | tf_op jit(solution)/shard_map/all_to_all | solution.py:32
  130.3 0.1 fusion.45
  130.4 0.7 broadcast_in_dim.116
  131.1 4.2 %all-to-all-start.3 = ((f32[32,8,8]{2,1,0:T(8,128)}), f32[32,8,8]{2,1,0:T(8,128)S(1)}, u32[]{:S(2)}, u32[]{:S(2)}) async-start(f32[32,8,8]{2,1,0:T(8,128)} %broadcast_in_dim.116), calls=%async_computation.3 | async-start | bytes 262144 | tf_op jit(solution)/shard_map/all_to_all | solution.py:32
  135.4 7.7 %all-to-all-done.3 = f32[32,8,8]{2,1,0:T(8,128)S(1)} async-done(((f32[32,8,8]{2,1,0:T(8,128)}), f32[32,8,8]{2,1,0:T(8,128)S(1)}, u32[]{:S(2)}, u32[]{:S(2)}) %all-to-all-start.3) | async-done | bytes 8224 | tf_op jit(solution)/shard_map/all_to_all | solution.py:32
  143.1 0.2 select_reduce_fusion.2
  143.4 0.2 convolution_convert_fusion.2
  143.6 9.0 %all_to_all.41 = bf16[1,8,4,192]{3,2,0,1:T(4,128)(2,1)S(1)} all-to-all(bf16[1,8,4,192]{3,2,0,1:T(4,128)(2,1)S(1)} %bitcast.68), channel_id=1, replica_groups=mesh['row'=32,'col'=8] {'col'}, dimensions={1} | all-to-all | bytes 24576 | tf_op jit(solution)/shard_map/all_to_all | solution.py:197
  152.6 16.3 %all_to_all.42 = bf16[32,1,32,192]{3,2,1,0:T(8,128)(2,1)S(1)} all-to-all(bf16[32,1,32,192]{3,2,1,0:T(8,128)(2,1)S(1)} %broadcast_in_dim.122), channel_id=1, replica_groups=mesh['row'=32,'col'=8] {'row'}, dimensions={0} | all-to-all | bytes 786432 | tf_op jit(solution)/shard_map/all_to_all | solution.py:32
  168.9 1.1 copy.56
  170.0 1.7 reshape.225
  171.7 3.1 %fusion.4 = f32[32,256]{1,0:T(8,128)} fusion(bf16[32,6144]{1,0:T(8,128)(2,1)S(1)} %reshape.225, bf16[1,6144,256]{2,1,0:T(8,128)(2,1)} %param.35), kind=kOutput, calls=%fused_computation.7 | convolution fusion | flops 100663296 | bytes 3571712 | tf_op jit(solution)/shard_map/emd,edf->emf/dot_general | solution.py:201
  174.8 4.5 %fusion = bf16[6144,32]{0,1:T(8,128)(2,1)} fusion(bf16[1,256,6144]{2,1,0:T(8,128)(2,1)S(1)} %copy-done, bf16[32,6144]{1,0:T(8,128)(2,1)S(1)} %reshape.225, bf16[1,6144,256]{2,1,0:T(8,128)(2,1)} %param.36, f32[32,256]{1,0:T(8,128)} %fusion.4), kind=kOutput, calls=%fused_computation.3 | convolution fusion | flops 201572352 | bytes 7110656 | tf_op jit(solution)/shard_map/rsw,rwp->prs/dot_general | solution.py:204
  179.3 2.4 %convert_element_type.82 = bf16[32,192,32]{1,0,2:T(8,128)(2,1)} reshape(bf16[6144,32]{0,1:T(8,128)(2,1)} %fusion) | data formatting | bytes 786432 | tf_op jit(solution)/shard_map/convert_element_type | solution.py:208
  181.8 1.3 copy.57
  183.1 15.1 %all_to_all.43 = bf16[32,192,32]{1,2,0:T(8,128)(2,1)} all-to-all(bf16[32,192,32]{1,2,0:T(8,128)(2,1)S(1)} %copy.57), channel_id=1, replica_groups=mesh['row'=32,'col'=8] {'row'}, dimensions={0} | all-to-all | bytes 786432 | tf_op jit(solution)/shard_map/all_to_all | solution.py:56
  198.2 1.1 reduce_sum.125
  199.4 9.0 %all_to_all.44 = bf16[192,1,8,4]{0,3,1,2:T(4,128)(2,1)S(1)} all-to-all(bf16[192,1,8,4]{0,3,1,2:T(4,128)(2,1)S(1)} %bitcast.69), channel_id=1, replica_groups=mesh['row'=32,'col'=8] {'col'}, dimensions={2} | all-to-all | bytes 24576 | tf_op jit(solution)/shard_map/all_to_all | solution.py:217
  208.4 0.7 fusion.18
  (45 shorter events, 1.4 us)
Async XLA Ops:
  6.5 168.3 %copy-start = (bf16[1,256,6144]{2,1,0:T(8,128)(2,1)S(1)}, bf16[1,256,6144]{2,1,0:T(8,128)(2,1)}, u32[]{:S(2)}) copy-start(bf16[1,256,6144]{2,1,0:T(8,128)(2,1)} %param.37) | copy-start | bytes 9437188
  6.5 65.4 %all-gather.2.cloned.1.call-start = ((), (), s32[]{:S(2)}) async-start(), calls=%async_computation.8 | async-start | bytes 8650752 | tf_op jit(solution)/shard_map/all_gather | solution.py:23
  81.5 12.6 %copy-start.4 = (s32[8,2]{0,1:T(2,128)S(1)}, s32[8,2]{0,1:T(2,128)}, u32[]{:S(2)}) copy-start(s32[8,2]{0,1:T(2,128)} %param.34) | copy-start | bytes 196
  85.2 2.4 %copy-start.1 = (bf16[2,2048,128]{2,1,0:T(8,128)(2,1)S(1)}, bf16[2,2048,128]{2,1,0:T(8,128)(2,1)}, u32[]{:S(2)}) copy-start(bf16[2,2048,128]{2,1,0:T(8,128)(2,1)} %param.25) | copy-start | bytes 3145732
  85.2 32.0 %copy-start.2 = (bf16[8,192]{1,0:T(8,128)(2,1)S(1)}, bf16[8,192]{1,0:T(8,128)(2,1)}, u32[]{:S(2)}) copy-start(bf16[8,192]{1,0:T(8,128)(2,1)} %param.20) | copy-start | bytes 9220
  85.2 45.1 %copy-start.5 = (f32[192]{0:T(256)S(1)}, f32[192]{0:T(256)}, u32[]{:S(2)}) copy-start(f32[192]{0:T(256)} %param.32) | copy-start | bytes 2308
  85.2 45.1 %copy-start.3 = (bf16[192,8]{0,1:T(8,128)(2,1)S(1)}, bf16[192,8]{0,1:T(8,128)(2,1)}, u32[]{:S(2)}) copy-start(bf16[192,8]{0,1:T(8,128)(2,1)} %param.33) | copy-start | bytes 9220
  88.6 12.9 %all-to-all-start = ((bf16[32,2,768]{2,1,0:T(2,128)(2,1)}), bf16[32,2,768]{2,1,0:T(2,128)(2,1)S(1)}, u32[]{:S(2)}, u32[]{:S(2)}) async-start(bf16[32,2,768]{2,1,0:T(2,128)(2,1)} %broadcast_in_dim.114), calls=%async_computation | async-start | bytes 196608 | tf_op jit(solution)/shard_map/all_to_all | solution.py:32
  103.4 13.7 %all-to-all-start.1 = ((bf16[8,8,192]{2,1,0:T(8,128)(2,1)}), bf16[8,8,192]{2,1,0:T(8,128)(2,1)S(1)}, u32[]{:S(2)}, u32[]{:S(2)}) async-start(bf16[8,8,192]{2,1,0:T(8,128)(2,1)} %fusion.11), calls=%async_computation.1 | async-start | bytes 65536 | tf_op jit(solution)/shard_map/all_to_all | solution.py:56
  117.9 12.3 %all-to-all-start.2 = ((f32[32,1,8]{2,1,0:T(1,128)}), f32[32,1,8]{2,1,0:T(1,128)S(1)}, u32[]{:S(2)}, u32[]{:S(2)}) async-start(f32[32,1,8]{2,1,0:T(1,128)} %broadcast_in_dim.115), calls=%async_computation.2 | async-start | bytes 32768 | tf_op jit(solution)/shard_map/all_to_all | solution.py:32
  131.1 12.0 %all-to-all-start.3 = ((f32[32,8,8]{2,1,0:T(8,128)}), f32[32,8,8]{2,1,0:T(8,128)S(1)}, u32[]{:S(2)}, u32[]{:S(2)}) async-start(f32[32,8,8]{2,1,0:T(8,128)} %broadcast_in_dim.116), calls=%async_computation.3 | async-start | bytes 262144 | tf_op jit(solution)/shard_map/all_to_all | solution.py:32
Sparse Core Ops, SparseCore 0:
  9.9 61.9 all-gather.1
where the time goes:
time: 217 us; the launch traced here: 216 us
  waiting for transfers between devices  85.4 us (39%)
  blocking collectives  49.4 us (23%)
  local copies, waits for them, and re-layouts  24.7 us (11%)
  starting transfers between devices  21.6 us (10%)
  matrix products  13.8 us (6%)
  between operations  13.5 us (6%)
  other arithmetic  7.42 us (3%)
    all_gather x1, waiting for transfers between devices, in_one_piece(): filled, at, done = (lax.all_gather(both, axis, axis=dim, tiled=True), 0, [])  56.8 us
    all_to_all x3, waiting for transfers between devices, sent_to_all(): lax.all_to_all(jnp.broadcast_to(value[None], (size, *value.shape)), axis,...  21.8 us
    all_to_all x1, blocking collectives, sent_to_all(): lax.all_to_all(jnp.broadcast_to(value[None], (size, *value.shape)), axis,...  16.3 us
    all_to_all x1, blocking collectives, summed_on_arrival(): lax.all_to_all(parts, axis, split_axis=0, concat_axis=0, tiled=True)  15.1 us
    all_to_all x3, starting transfers between devices, sent_to_all(): lax.all_to_all(jnp.broadcast_to(value[None], (size, *value.shape)), axis,...  14.9 us
    all_to_all x1, blocking collectives, body(): lax.all_to_all(outgoing, 'col', split_axis=1, concat_axis=1, tiled=True)  8.99 us
    all_to_all x1, blocking collectives, body(): lax.all_to_all(outputs, 'col', split_axis=2, concat_axis=2, tiled=True)  8.98 us
    all_to_all x1, waiting for transfers between devices, summed_on_arrival(): lax.all_to_all(parts, axis, split_axis=0, concat_axis=0, tiled=True)  6.86 us
  transfers between devices with their start and end apart: 5, of which 5 were waited for; matrix products, arithmetic and copies ran while one was open for 3% of the time, Pallas kernels for 0%

commit v1 on v0

v1 whole, which is shorter than its diff:
```python
import functools
import math

import jax
import jax.numpy as jnp
from jax import lax
from jax.experimental import pallas as pl
from jax.experimental.pallas import tpu as pltpu
from jax.sharding import PartitionSpec as P

D = 6144
HQ = 48
KVH = 8
HD = 128
GROUP = HQ // KVH
EXPERTS = 8
CAP = 4
NEG = -1e30
EPS = 1e-05
NX, NY, NCORE = 4, 4, 2
NR = NX * NY * NCORE
NC = 8
SEQS = 64
BLOCK = SEQS // NC
SLOTS = 4
PAGE = 128
KEYS = SLOTS * PAGE
CTX = 2048
WIDTH = D // NR
WPAD = 256
FSLICE = 256
ROWS = NC * CAP
HROWS = 16
SCALE = 1.0 / math.sqrt(HD)
F32 = jnp.float32
BF16 = jnp.bfloat16

ROW_PEERS = [
    (dx, dy, dc)
    for dx in range(NX)
    for dy in range(NY)
    for dc in range(NCORE)
    if (dx, dy, dc) != (0, 0, 0)
]
ROW_PEERS.sort(key=lambda t: -(min(t[0], NX - t[0]) + min(t[1], NY - t[1]) + 0.5 * t[2]))
COL_PEERS = sorted(range(1, NC), key=lambda d: -min(d, NC - d))


def iota(shape, dim):
    return lax.broadcasted_iota(jnp.int32, shape, dim)


def nt_dot(a, b):
    return lax.dot_general(a, b, (((1,), (1,)), ((), ())), preferred_element_type=F32)


def dot(a, b):
    return jnp.dot(a, b, preferred_element_type=F32)


def kernel(
    lengths,
    resident_s,
    experts_s,
    hidden,
    queries,
    new_keys,
    new_values,
    page_table,
    resident,
    gain,
    router,
    cache_keys,
    cache_values,
    prefix_keys,
    prefix_values,
    out_weight,
    gate_weight,
    up_weight,
    down_weight,
    out,
    kc,
    vc,
    pk,
    pv,
    wo,
    wg,
    wu,
    wd,
    qsend,
    qall,
    psend,
    prec,
    asend,
    aall,
    tsend,
    trec,
    xsend,
    xall,
    ysend,
    yrec,
    zsend,
    zrec,
    hsend,
    hrec,
    sel,
    cntk,
    disp,
    hot128,
    raug,
    gpad,
    hpad,
    pbs,
    hres,
    local_sem,
    send_sem,
    recv_sem,
):
    r = lax.axis_index("row")
    c = lax.axis_index("col")
    rx, ry, rc = r // (NY * NCORE), (r // NCORE) % NY, r % NCORE

    def row_peer(t):
        dx, dy, dc = t
        return ((rx + dx) % NX) * (NY * NCORE) + ((ry + dy) % NY) * NCORE + (rc + dc) % NCORE

    def col_peer(d):
        return (c + d) % NC

    barrier = pltpu.get_barrier_semaphore()
    for t in ROW_PEERS:
        pl.semaphore_signal(barrier, inc=1, device_id={"row": row_peer(t), "col": c}, device_id_type=pl.DeviceIdType.MESH)
    for d in COL_PEERS:
        pl.semaphore_signal(barrier, inc=1, device_id={"row": r, "col": col_peer(d)}, device_id_type=pl.DeviceIdType.MESH)

    loads = [
        pltpu.make_async_copy(s, t, local_sem.at[i])
        for i, (s, t) in enumerate(
            (
                (prefix_keys.at[0], pk),
                (prefix_values.at[0], pv),
                (cache_keys, kc),
                (cache_values, vc),
                (out_weight, wo),
                (gate_weight.at[0], wg),
                (up_weight.at[0], wu),
                (down_weight.at[0], wd),
            )
        )
    ]
    for load in loads:
        load.start()

    def to_row(phase, src_of, dst):
        for t in ROW_PEERS:
            peer = row_peer(t)
            pltpu.make_async_remote_copy(
                src_ref=src_of(peer),
                dst_ref=dst.at[r],
                send_sem=send_sem.at[phase],
                recv_sem=recv_sem.at[phase],
                device_id={"row": peer, "col": c},
                device_id_type=pl.DeviceIdType.MESH,
            ).start()

    def to_col(phase, src_of, dst):
        for d in COL_PEERS:
            peer = col_peer(d)
            pltpu.make_async_remote_copy(
                src_ref=src_of(peer),
                dst_ref=dst.at[c],
                send_sem=send_sem.at[phase],
                recv_sem=recv_sem.at[phase],
                device_id={"row": r, "col": peer},
                device_id_type=pl.DeviceIdType.MESH,
            ).start()

    def wait_for(sem, buffer, count):
        part = buffer.at[pl.ds(0, count)]
        pltpu.make_async_copy(part, part, sem).wait()

    q = queries[...].astype(F32)
    qrows = jnp.concatenate(
        [q[:, g * HD : (g + 1) * HD] for g in range(GROUP)] + [jnp.zeros((HROWS - 2 * GROUP, HD), F32)], axis=0
    )
    q16 = qrows.astype(BF16)
    qsend[...] = q16
    qall[r] = q16
    e_i, b_i = iota((EXPERTS, 128), 0), iota((EXPERTS, 128), 1)
    hot = jnp.zeros((EXPERTS, 128), F32)
    for b in range(BLOCK):
        named = (e_i == experts_s[b, 0]) | (e_i == experts_s[b, 1])
        hot = jnp.where(named & (b_i == c * BLOCK + b), 1.0, hot)
    hsend[...] = hot
    hrec[c] = hot

    pl.semaphore_wait(barrier, len(ROW_PEERS) + len(COL_PEERS))
    to_row(0, lambda peer: qsend, qall)
    to_col(1, lambda peer: hsend, hrec)

    lane64 = iota((SEQS, 128), 1)
    table = page_table[...]
    res = resident[...]
    flat = iota(res.shape, 0) * SLOTS + iota(res.shape, 1)
    for j in range(SLOTS):
        page = resident_s[r, j]
        earlier = jnp.sum(jnp.where((res == page) & (flat < r * SLOTS + j), 1.0, 0.0), keepdims=True)
        times = jnp.sum(jnp.where(table == page, 1.0, 0.0), axis=1, keepdims=True)
        times = jnp.where(earlier > 0.0, 0.0, times)
        cntk[:, j * PAGE : (j + 1) * PAGE] = jnp.broadcast_to(times, (SEQS, PAGE)).astype(BF16)
    for g in range(GROUP):
        want, have = iota((SEQS, NR * HROWS), 0), iota((SEQS, NR * HROWS), 1)
        there = (want // 2) * HROWS + 2 * g + want % 2
        sel[g * SEQS : (g + 1) * SEQS, :] = jnp.where(have == there, 1.0, 0.0).astype(BF16)
    place = jnp.where(
        (iota((EXPERTS, WPAD), 1) >= WIDTH) & (iota((EXPERTS, WPAD), 1) < WIDTH + 48)
        & ((iota((EXPERTS, WPAD), 1) - WIDTH) % 16 == iota((EXPERTS, WPAD), 0)), 1.0, 0.0
    ).astype(BF16)
    raug[...] = dot(router[...], place).astype(BF16)
    gpad[...] = jnp.zeros_like(gpad)
    gpad[0:1, 0:WIDTH] = gain[...]
    hpad[...] = jnp.zeros_like(hpad)
    hpad[:, 0:WIDTH] = hidden[...].astype(F32)
    pbs[...] = jnp.zeros_like(pbs)
    hot128[...] = jnp.zeros_like(hot128)

    loads[2].wait()
    odd = iota((HROWS, 1), 0) % 2 == 1
    own = [nt_dot(q16, kc[s]) for s in range(2)]
    scores = jnp.where(odd, own[1], own[0]) * SCALE
    length = jnp.where(odd, lengths[1], lengths[0])
    scores = jnp.where(iota((HROWS, CTX), 1) < length, scores, NEG)
    fresh_k = jnp.where(odd, new_keys[1:2, :].astype(F32), new_keys[0:1, :].astype(F32))
    fresh_v = jnp.where(odd, new_values[1:2, :].astype(F32), new_values[0:1, :].astype(F32))
    fresh = jnp.sum(qrows * fresh_k, axis=1, keepdims=True) * SCALE
    peak = jnp.maximum(jnp.max(scores, axis=1, keepdims=True), fresh)
    expo = jnp.exp(scores - peak)
    fresh_e = jnp.exp(fresh - peak)
    own_total = jnp.sum(expo, axis=1, keepdims=True) + fresh_e
    loads[3].wait()
    mixed = (
        dot(jnp.where(odd, 0.0, expo).astype(BF16), vc[0])
        + dot(jnp.where(odd, expo, 0.0).astype(BF16), vc[1])
        + fresh_e.astype(BF16).astype(F32) * fresh_v
    )
    own_peak = peak

    loads[0].wait()
    loads[1].wait()
    wait_for(recv_sem.at[0], qall, NR - 1)
    CH = 8
    for i in range(NR // CH):
        n = CH * HROWS
        qs = qall[i * CH : (i + 1) * CH].reshape(n, HD)
        row = iota((n, SEQS), 0)
        member = (i * CH + row // HROWS) * 2 + row % 2 == iota((n, SEQS), 1)
        times = dot(jnp.where(member, 1.0, 0.0).astype(BF16), cntk[...])
        s = nt_dot(qs, pk[...].reshape(KEYS, HD)) * SCALE
        s = jnp.where(times > 0.0, s, NEG)
        m = jnp.max(s, axis=1, keepdims=True)
        e = jnp.exp(s - m) * times
        l = jnp.sum(e, axis=1, keepdims=True)
        o = dot(e.astype(BF16), pv[...].reshape(KEYS, HD))
        some = l > 0.0
        safe = jnp.where(some, l, 1.0)
        o = o / safe
        lse = jnp.where(some, m + jnp.log(safe), NEG)
        k_i = iota((n, HD), 0) % HROWS
        diag = jnp.where(k_i == iota((n, HD), 1), lse, 0.0)
        across = jnp.sum(diag.reshape(CH, HROWS, HD), axis=1, keepdims=True)
        across = jnp.broadcast_to(across, (CH, HROWS, HD)).reshape(n, HD)
        hi = across.astype(BF16).astype(F32)
        mid = (across - hi).astype(BF16).astype(F32)
        lo = across - hi - mid
        tail = jnp.where(k_i == 12, hi, jnp.where(k_i == 13, mid, jnp.where(k_i == 14, lo, 0.0)))
        psend[i * CH : (i + 1) * CH] = jnp.where(k_i < 12, o, tail).astype(BF16).reshape(CH, HROWS, HD)
    prec[r] = psend[r]
    to_row(2, lambda peer: psend.at[peer], prec)

    wait_for(recv_sem.at[1], hrec, NC - 1)
    hot = jnp.sum(hrec[...], axis=0)
    hot128[0:EXPERTS, :] = hot
    u0, u1 = iota((128, 128), 0), iota((128, 128), 1)
    before = jnp.where((u0 < u1) & (u0 // BLOCK == u1 // BLOCK), 1.0, 0.0).astype(BF16)
    rank = dot(hot.astype(BF16), before)
    d_r, d_l = iota((ROWS, 128), 0), iota((ROWS, 128), 1)
    for e in range(EXPERTS):
        hit = (
            (hot[e : e + 1, :] > 0.0)
            & (rank[e : e + 1, :] == (d_r % CAP).astype(F32))
            & (d_l // BLOCK == d_r // CAP)
        )
        home = d_l % SEQS == e * BLOCK + d_r % BLOCK
        low = jnp.where(hit & (d_l < SEQS), 1.0, 0.0) + jnp.where(
            home & (d_l >= SEQS) & (d_r // BLOCK == 0), 1.0, 0.0
        )
        high = jnp.where(home & (d_r // BLOCK == 1 + d_l // SEQS), 1.0, 0.0)
        disp[e * ROWS : (e + 1) * ROWS, 0:128] = low.astype(BF16)
        disp[e * ROWS : (e + 1) * ROWS, 128:256] = high.astype(BF16)

    wait_for(recv_sem.at[2], prec, NR - 1)
    parts = prec[...].astype(F32)
    lrow = parts[:, 12:13, :] + parts[:, 13:14, :] + parts[:, 14:15, :]
    on_diag = iota((NR, HROWS, HD), 1) == iota((NR, HROWS, HD), 2)
    lse = jnp.sum(jnp.where(on_diag, jnp.broadcast_to(lrow, (NR, HROWS, HD)), 0.0), axis=2, keepdims=True)
    lse = jnp.where(iota((NR, HROWS, 1), 1) < 12, lse, NEG)
    top = jnp.maximum(jnp.max(lse, axis=0), own_peak)
    w = jnp.exp(lse - top[None])
    w_own = jnp.exp(own_peak - top)
    total = jnp.sum(w, axis=0) + own_total * w_own
    mixed = jnp.sum(w * parts, axis=0) + mixed * w_own
    att = jnp.where(iota((HROWS, HD), 0) < 12, mixed / total, 0.0).astype(BF16)
    asend[...] = att
    aall[r] = att
    to_row(3, lambda peer: asend, aall)

    loads[4].wait()
    wait_for(recv_sem.at[3], aall, NR - 1)
    picked = dot(sel[...], aall[...].reshape(NR * HROWS, HD)).astype(BF16)
    projected = dot(picked[0:SEQS], wo[0:HD, :])
    for g in range(1, GROUP):
        projected = projected + dot(picked[g * SEQS : (g + 1) * SEQS], wo[g * HD : (g + 1) * HD, :])
    pbs[:, 0:WIDTH] = projected
    plain = pbs[...]
    here = jnp.where(iota((SEQS, BLOCK), 0) == c * BLOCK + iota((SEQS, BLOCK), 1), 1.0, 0.0).astype(BF16)
    with_hidden = plain + dot(here, hpad[...].astype(BF16))
    lane = iota((SEQS, WPAD), 1)
    moved = [jnp.where(lane >= WIDTH, pltpu.roll(plain, WIDTH - 64 * i, 1), 0.0) for i in range(3)]
    stacked = jnp.concatenate([with_hidden] + moved, axis=0).astype(BF16)
    tsend[...] = dot(disp[...], stacked).astype(BF16).reshape(NC, ROWS, WPAD)
    trec[c] = tsend[c]
    to_col(4, lambda peer: tsend.at[peer], trec)

    wait_for(recv_sem.at[4], trec, NC - 1)
    resid = jnp.sum(trec[...].astype(F32), axis=0)
    lane8 = iota((BLOCK, WPAD), 1)
    home = hpad[...]
    for i in range(3):
        piece = pltpu.roll(resid[i * BLOCK : (i + 1) * BLOCK, :], (64 * i + 64) % WPAD, 1)
        home = home + jnp.where(lane8 // 64 == i, piece, 0.0)
    hres[...] = home
    lane32 = iota((ROWS, WPAD), 1)
    squares = jnp.sum(jnp.where(lane32 < WIDTH, resid * resid, 0.0), axis=1, keepdims=True)
    x = resid * gpad[0:1, :]
    stats = dot(x[:, 0:WIDTH].astype(BF16), raug[...])
    stats = stats + jnp.where((lane32 >= WIDTH) & ((lane32 - WIDTH) % 16 == 8), squares, 0.0)
    hi = stats.astype(BF16).astype(F32)
    mid = (stats - hi).astype(BF16).astype(F32)
    lo = stats - hi - mid
    x = jnp.where(lane32 < WIDTH, x, jnp.where(lane32 < WIDTH + 16, hi, jnp.where(lane32 < WIDTH + 32, mid, jnp.where(lane32 < WIDTH + 48, lo, 0.0))))
    x = x.astype(BF16)
    xsend[...] = x
    xall[r] = x
    to_row(5, lambda peer: xsend, xall)

    loads[5].wait()
    loads[6].wait()
    mine = disp[pl.ds(pl.multiple_of(c * ROWS, ROWS), ROWS), 0:128]
    mine = jnp.where(iota((ROWS, 128), 1) < SEQS, mine.astype(F32), 0.0)
    wait_for(recv_sem.at[5], xall, NR - 1)

    def expert_step(i, carry):
        g, u, st = carry
        xi = xall[i]
        rows = pl.ds(pl.multiple_of(i * WIDTH, 64), WIDTH)
        g = g + dot(xi[:, 0:WIDTH], wg[rows, :])
        u = u + dot(xi[:, 0:WIDTH], wu[rows, :])
        st = st + xi[:, 128:256].astype(F32)
        return g, u, st

    inner_gate, inner_up, st = lax.fori_loop(
        0, NR, expert_step,
        (jnp.zeros((ROWS, FSLICE), F32), jnp.zeros((ROWS, FSLICE), F32), jnp.zeros((ROWS, 128), F32)),
    )
    st = st + pltpu.roll(st, 112, 1) + pltpu.roll(st, 96, 1)
    st = pltpu.roll(st, 64, 1)
    lane128 = iota((ROWS, 128), 1)
    squares = jnp.sum(jnp.where(lane128 == 8, st, 0.0), axis=1, keepdims=True)
    inverse = lax.rsqrt(squares / D + EPS)
    pair = nt_dot(mine.astype(BF16), hot128[...].astype(BF16))
    logits = st * inverse
    own_logit = jnp.sum(jnp.where(lane128 == c, logits, 0.0), axis=1, keepdims=True)
    other = jnp.sum(jnp.where((pair > 0.0) & (lane128 != c), logits, 0.0), axis=1, keepdims=True)
    share = 1.0 / (1.0 + jnp.exp(other - own_logit))
    inner_gate = inner_gate * inverse
    inner_up = inner_up * inverse
    act = (inner_gate / (1.0 + jnp.exp(-inner_gate)) * inner_up * share).astype(BF16)
    loads[7].wait()
    for k in range(NR // 2):
        y = dot(act, wd[:, k * 2 * WIDTH : (k + 1) * 2 * WIDTH])
        ysend[2 * k] = y[:, 0:WPAD].astype(BF16)
        ysend[2 * k + 1] = pltpu.roll(y[:, 128 : 128 + WPAD], WPAD - 64, 1).astype(BF16)
    yrec[r] = ysend[r]
    to_row(6, lambda peer: ysend.at[peer], yrec)

    wait_for(recv_sem.at[6], yrec, NR - 1)
    ysum = lax.fori_loop(0, NR, lambda i, acc: acc + yrec[i].astype(F32), jnp.zeros((ROWS, WPAD), F32))
    back = lax.dot_general(
        mine.astype(BF16), ysum.astype(BF16), (((0,), (0,)), ((), ())), preferred_element_type=F32
    )
    for i in range(NC):
        both = jnp.concatenate(
            [back[i * BLOCK : (i + 1) * BLOCK, 0:128], back[i * BLOCK : (i + 1) * BLOCK, 128:256]], axis=0
        )
        zsend[i] = both.astype(BF16)
    zrec[c] = zsend[c]
    to_col(7, lambda peer: zsend.at[peer], zrec)
    wait_for(recv_sem.at[7], zrec, NC - 1)
    z = jnp.sum(zrec[...].astype(F32), axis=0)
    final = hres[...]
    out[:, 0:128] = (final[:, 0:128] + z[0:BLOCK]).astype(out.dtype)
    out[:, 128:WIDTH] = (final[:, 128:WIDTH] + z[BLOCK:, 0 : WIDTH - 128]).astype(out.dtype)

    wait_for(send_sem.at[0], qall, NR - 1)
    wait_for(send_sem.at[1], hrec, NC - 1)
    wait_for(send_sem.at[2], prec, NR - 1)
    wait_for(send_sem.at[3], aall, NR - 1)
    wait_for(send_sem.at[4], trec, NC - 1)
    wait_for(send_sem.at[5], xall, NR - 1)
    wait_for(send_sem.at[6], yrec, NR - 1)
    wait_for(send_sem.at[7], zrec, NC - 1)


def body(
    hidden,
    queries,
    new_keys,
    new_values,
    cache_keys,
    cache_values,
    lengths,
    page_table,
    resident,
    prefix_keys,
    prefix_values,
    out_weight,
    norm_gain,
    router_weight,
    experts,
    gate_weight,
    up_weight,
    down_projection_weight,
):
    smem = pl.BlockSpec(memory_space=pltpu.SMEM)
    vmem = pl.BlockSpec(memory_space=pltpu.VMEM)
    anyw = pl.BlockSpec(memory_space=pl.ANY)
    return pl.pallas_call(
        kernel,
        out_shape=jax.ShapeDtypeStruct((BLOCK, WIDTH), BF16),
        in_specs=[smem] * 3 + [vmem] * 8 + [anyw] * 8,
        out_specs=vmem,
        scratch_shapes=[
            pltpu.VMEM((2, CTX, HD), BF16),
            pltpu.VMEM((2, CTX, HD), BF16),
            pltpu.VMEM((SLOTS, PAGE, HD), BF16),
            pltpu.VMEM((SLOTS, PAGE, HD), BF16),
            pltpu.VMEM((GROUP * HD, WIDTH), BF16),
            pltpu.VMEM((D, FSLICE), BF16),
            pltpu.VMEM((D, FSLICE), BF16),
            pltpu.VMEM((FSLICE, D), BF16),
            pltpu.VMEM((HROWS, HD), BF16),
            pltpu.VMEM((NR, HROWS, HD), BF16),
            pltpu.VMEM((NR, HROWS, HD), BF16),
            pltpu.VMEM((NR, HROWS, HD), BF16),
            pltpu.VMEM((HROWS, HD), BF16),
            pltpu.VMEM((NR, HROWS, HD), BF16),
            pltpu.VMEM((NC, ROWS, WPAD), BF16),
            pltpu.VMEM((NC, ROWS, WPAD), BF16),
            pltpu.VMEM((ROWS, WPAD), BF16),
            pltpu.VMEM((NR, ROWS, WPAD), BF16),
            pltpu.VMEM((NR, ROWS, WPAD), BF16),
            pltpu.VMEM((NR, ROWS, WPAD), BF16),
            pltpu.VMEM((NC, 2 * BLOCK, 128), BF16),
            pltpu.VMEM((NC, 2 * BLOCK, 128), BF16),
            pltpu.VMEM((EXPERTS, 128), F32),
            pltpu.VMEM((NC, EXPERTS, 128), F32),
            pltpu.VMEM((GROUP * SEQS, NR * HROWS), BF16),
            pltpu.VMEM((SEQS, KEYS), BF16),
            pltpu.VMEM((NC * ROWS, WPAD), BF16),
            pltpu.VMEM((128, 128), F32),
            pltpu.VMEM((WIDTH, WPAD), BF16),
            pltpu.VMEM((8, WPAD), F32),
            pltpu.VMEM((BLOCK, WPAD), F32),
            pltpu.VMEM((SEQS, WPAD), F32),
            pltpu.VMEM((BLOCK, WPAD), F32),
            pltpu.SemaphoreType.DMA((8,)),
            pltpu.SemaphoreType.DMA((8,)),
            pltpu.SemaphoreType.DMA((8,)),
        ],
        compiler_params=pltpu.CompilerParams(
            collective_id=0, has_side_effects=True, vmem_limit_bytes=48 * 1024 * 1024
        ),
        name="layer",
    )(
        lengths,
        resident,
        experts,
        hidden,
        queries,
        new_keys,
        new_values,
        page_table,
        resident,
        norm_gain.reshape(1, WIDTH),
        router_weight,
        cache_keys,
        cache_values,
        prefix_keys,
        prefix_values,
        out_weight,
        gate_weight,
        up_weight,
        down_projection_weight,
    )


def solution(mesh):
    in_specs = (
        P("col", "row"),
        P("row", "col"),
        P("row", "col"),
        P("row", "col"),
        P("row", None, "col"),
        P("row", None, "col"),
        P("row"),
        P(),
        P(),
        P("row", None, None, "col"),
        P("row", None, None, "col"),
        P("col", "row"),
        P("row"),
        P("row", None),
        P("col", None),
        P("col", None, "row"),
        P("col", None, "row"),
        P("col", "row", None),
    )
    return jax.shard_map(body, mesh=mesh, in_specs=in_specs, out_specs=P("col", "row"), check_vma=False)
```

time: 217 us -> 74.3 us (0.34)
  waiting for transfers between devices: 85.4 us -> 0 us
  Pallas kernels: 0 us -> 58.8 us
  blocking collectives: 49.4 us -> 0 us
  starting transfers between devices: 21.6 us -> 0 us
  matrix products: 13.8 us -> 0 us
  between operations: 13.5 us -> 0.04 us
  local copies, waits for them, and re-layouts: 24.7 us -> 15 us
  other arithmetic: 7.42 us -> 0 us
    pallas_call x0 -> x1, Pallas kernels: none -> 58.8 us  [body(): pl.pallas_call(kernel, out_shape=jax.ShapeDtypeStruct((BLOCK, WIDTH), BF1...]
    all_gather x1 -> x0, waiting for transfers between devices: 56.8 us -> none  [in_one_piece(): filled, at, done = (lax.all_gather(both, axis, axis=dim, tiled=True), 0, [])]
    all_to_all x4 -> x0, blocking collectives: 49.4 us -> none  [the longest x1 16.3 us: sent_to_all(): lax.all_to_all(jnp.broadcast_to(value[None], (size, *value.shape)), axis,...]
    all_to_all x4 -> x0, waiting for transfers between devices: 28.7 us -> none  [the longest x3 21.8 us: sent_to_all(): lax.all_to_all(jnp.broadcast_to(value[None], (size, *value.shape)), axis,...]
    all_to_all x4 -> x0, starting transfers between devices: 21.6 us -> none  [the longest x3 14.9 us: sent_to_all(): lax.all_to_all(jnp.broadcast_to(value[None], (size, *value.shape)), axis,...]
    unnamed x15 -> x28, local copies, waits for them, and re-layouts: 0.88 us -> 15 us
    dot_general x11 -> x0, matrix products: 13.8 us -> none  [the longest x1 4.48 us: body(): jnp.einsum('rsw,rwp->prs', activated_hidden, down_projection_weight, pref...]
    gather x2 -> x0, local copies, waits for them, and re-layouts: 7.21 us -> none  [the longest x1 3.62 us: body(): jnp.take(pool_values, places, axis=0).reshape(seq_row, -1, kv_local, HD)]
  transfers between devices with their start and end apart: 5 -> 0, of which waited for: 5 -> 0; matrix products, arithmetic and copies ran while one was open for 3% -> 0% of each run, Pallas kernels for 0% -> 0%
where the time goes in v1:
time: 74.3 us; the launch traced here: 73.8 us
  Pallas kernels  58.8 us (79%)
  local copies, waits for them, and re-layouts  15 us (20%)
    pallas_call x1, Pallas kernels, body(): pl.pallas_call(kernel, out_shape=jax.ShapeDtypeStruct((BLOCK, WIDTH), BF1...  58.8 us
    unnamed x28, local copies, waits for them, and re-layouts  15 us

profile of v1, /device:TPU:1, one launch (start us, length us, event | category | flops | bytes accessed | tf_op | source)
XLA Modules:
  0.0 73.8 jit_solution(17953911375751287827)
XLA Ops:
  0.0 0.8 %copy.20.experts_s = s32[8,2]{1,0:T(8,128)S(1)} copy(s32[8,2]{0,1:T(2,128)} %param.32) | data formatting | bytes 128 | tf_op args[14]
  0.8 0.8 %copy.19.resident_s.resident = s32[32,4]{1,0:T(8,128)S(1)} copy(s32[32,4]{0,1:T(4,128)} %param.26) | data formatting | bytes 1024 | tf_op args[8]
  1.5 0.8 %copy.21.page_table = s32[64,8]{1,0:T(8,128)S(1)} copy(s32[64,8]{0,1:T(8,128)} %param.25) | data formatting | bytes 4096 | tf_op args[7]
  2.3 0.8 %copy.23.router = bf16[192,8]{1,0:T(8,128)(2,1)S(1)} copy(bf16[192,8]{0,1:T(8,128)(2,1)} %param.31) | data formatting | bytes 6144 | tf_op args[13]
  3.1 1.1 %copy.24.out_weight = bf16[768,192]{1,0:T(8,128)(2,1)S(1)} copy(bf16[768,192]{0,1:T(8,128)(2,1)} %param.29) | data formatting | bytes 589824 | tf_op args[11]
  4.2 0.0 copy-start
  4.3 1.9 %copy-done = bf16[1,6144,256]{2,1,0:T(8,128)(2,1)S(1)} copy-done((bf16[1,6144,256]{2,1,0:T(8,128)(2,1)S(1)}, bf16[1,6144,256]{2,1,0:T(8,128)(2,1)}, u32[]{:S(2)}) %copy-start) | copy-done | bytes 3145752
  6.1 0.0 copy-start.1
  6.1 1.2 %copy-done.1 = bf16[2,2048,128]{2,1,0:T(8,128)(2,1)S(1)} copy-done((bf16[2,2048,128]{2,1,0:T(8,128)(2,1)S(1)}, bf16[2,2048,128]{2,1,0:T(8,128)(2,1)}, u32[]{:S(2)}) %copy-start.1) | copy-done | bytes 1048600
  7.4 0.0 copy-start.2
  7.4 1.2 %copy-done.2 = bf16[2,2048,128]{2,1,0:T(8,128)(2,1)S(1)} copy-done((bf16[2,2048,128]{2,1,0:T(8,128)(2,1)S(1)}, bf16[2,2048,128]{2,1,0:T(8,128)(2,1)}, u32[]{:S(2)}) %copy-start.2) | copy-done | bytes 1048600
  8.6 0.0 copy-start.3
  8.6 0.9 %copy-done.3 = bf16[1,4,128,128]{3,2,1,0:T(8,128)(2,1)S(1)} copy-done((bf16[1,4,128,128]{3,2,1,0:T(8,128)(2,1)S(1)}, bf16[1,4,128,128]{3,2,1,0:T(8,128)(2,1)}, u32[]{:S(2)}) %copy-start.3) | copy-done | bytes 131096
  9.5 0.0 copy-start.4
  9.5 0.9 %copy-done.4 = bf16[1,4,128,128]{3,2,1,0:T(8,128)(2,1)S(1)} copy-done((bf16[1,4,128,128]{3,2,1,0:T(8,128)(2,1)S(1)}, bf16[1,4,128,128]{3,2,1,0:T(8,128)(2,1)}, u32[]{:S(2)}) %copy-start.4) | copy-done | bytes 131096
  10.4 0.0 copy-start.5
  10.4 0.7 copy-done.5
  11.1 0.0 copy-start.6
  11.1 0.7 copy-done.6
  11.8 0.0 copy-start.7
  11.8 0.7 copy-done.7
  12.5 0.0 copy-start.8
  12.5 0.7 copy-done.8
  13.1 0.0 copy-start.9
  13.1 0.7 copy-done.9
  13.8 0.0 copy-start.10
  13.8 0.7 copy-done.10
  14.4 58.8 %layer.1 = bf16[8,192]{1,0:T(8,128)(2,1)S(1)} custom-call(s32[2]{0:T(128)S(1)} %copy-done.8, s32[32,4]{1,0:T(8,128)S(1)} %copy.19.resident_s.resident, s32[8,2]{1,0:T(8,128)S(1)} %copy.20.experts_s, bf16[8,192]{1,0:T(8,128)(2,1)S(1)} %copy-done.5, bf16[2,768]{1,0:T(2,128)(2,1)S(1)} %copy-done.6, bf16[2,128]{1,0:T(2,128)(2,1)S(1)} %copy-done.9, ...), custom_call_target="tpu_custom_call" | custom-call | tf_op jit(solution)/shard_map/layer/pallas_call | solution.py:447
  73.2 0.6 copy.26
Async XLA Ops:
  4.2 1.9 %copy-start = (bf16[1,6144,256]{2,1,0:T(8,128)(2,1)S(1)}, bf16[1,6144,256]{2,1,0:T(8,128)(2,1)}, u32[]{:S(2)}) copy-start(bf16[1,6144,256]{2,1,0:T(8,128)(2,1)} %gate_weight.1) | copy-start | bytes 9437188
  6.1 1.2 %copy-start.1 = (bf16[2,2048,128]{2,1,0:T(8,128)(2,1)S(1)}, bf16[2,2048,128]{2,1,0:T(8,128)(2,1)}, u32[]{:S(2)}) copy-start(bf16[2,2048,128]{2,1,0:T(8,128)(2,1)} %cache_keys.1) | copy-start | bytes 3145732
  7.4 1.2 %copy-start.2 = (bf16[2,2048,128]{2,1,0:T(8,128)(2,1)S(1)}, bf16[2,2048,128]{2,1,0:T(8,128)(2,1)}, u32[]{:S(2)}) copy-start(bf16[2,2048,128]{2,1,0:T(8,128)(2,1)} %cache_values.1) | copy-start | bytes 3145732
  8.6 0.9 %copy-start.3 = (bf16[1,4,128,128]{3,2,1,0:T(8,128)(2,1)S(1)}, bf16[1,4,128,128]{3,2,1,0:T(8,128)(2,1)}, u32[]{:S(2)}) copy-start(bf16[1,4,128,128]{3,2,1,0:T(8,128)(2,1)} %prefix_keys.1) | copy-start | bytes 393220
  9.5 0.9 %copy-start.4 = (bf16[1,4,128,128]{3,2,1,0:T(8,128)(2,1)S(1)}, bf16[1,4,128,128]{3,2,1,0:T(8,128)(2,1)}, u32[]{:S(2)}) copy-start(bf16[1,4,128,128]{3,2,1,0:T(8,128)(2,1)} %prefix_values.1) | copy-start | bytes 393220
  10.4 0.7 copy-start.5
  11.1 0.7 copy-start.6
  11.8 0.7 copy-start.7
  12.5 0.7 copy-start.8
  13.1 0.7 copy-start.9
  13.8 0.7 copy-start.10

commit v2 on v1

v2 whole, which is shorter than its diff:
```python
import functools
import math

import jax
import jax.numpy as jnp
from jax import lax
from jax.experimental import pallas as pl
from jax.experimental.pallas import tpu as pltpu
from jax.sharding import PartitionSpec as P

D = 6144
HQ = 48
KVH = 8
HD = 128
GROUP = HQ // KVH
EXPERTS = 8
CAP = 4
NEG = -1e30
EPS = 1e-05
NX, NY, NCORE = 4, 4, 2
NR = NX * NY * NCORE
NC = 8
SEQS = 64
BLOCK = SEQS // NC
SLOTS = 4
PAGE = 128
KEYS = SLOTS * PAGE
CTX = 2048
WIDTH = D // NR
WPAD = 256
FSLICE = 256
ROWS = NC * CAP
HROWS = 16
SCALE = 1.0 / math.sqrt(HD)
F32 = jnp.float32
BF16 = jnp.bfloat16

ROW_PEERS = [
    (dx, dy, dc)
    for dx in range(NX)
    for dy in range(NY)
    for dc in range(NCORE)
    if (dx, dy, dc) != (0, 0, 0)
]
ROW_PEERS.sort(key=lambda t: -(min(t[0], NX - t[0]) + min(t[1], NY - t[1]) + 0.5 * t[2]))
PER_X = NY * NCORE
NEAR_FIRST = (0, 1, 3, 2)
ARRIVAL = (2, 1, 3, 0)
ORDER1 = (0, 1, 3, 2)
ORDER2 = (0, 1, 3, 2)
ORDER3 = (2, 1, 3, 0)
FAR_FIRST = (2, 1, 3, 0)
CHIP_PEERS = [t for t in ROW_PEERS if t[2] == 0]
CHIPS = NX * NY
COL_PEERS = sorted(range(1, NC), key=lambda d: -min(d, NC - d))


def iota(shape, dim):
    return lax.broadcasted_iota(jnp.int32, shape, dim)


def nt_dot(a, b):
    return lax.dot_general(a, b, (((1,), (1,)), ((), ())), preferred_element_type=F32)


def dot(a, b):
    return jnp.dot(a, b, preferred_element_type=F32)


def kernel(
    lengths_h,
    resident_h,
    experts_h,
    hidden_h,
    queries_h,
    new_keys_h,
    new_values_h,
    page_table_h,
    gain_h,
    router_h,
    cache_keys,
    cache_values,
    prefix_keys,
    prefix_values,
    out_weight,
    gate_weight,
    up_weight,
    down_weight,
    out,
    lengths,
    resident_s,
    experts_s,
    hidden,
    queries,
    new_keys,
    new_values,
    page_table,
    resident,
    gain,
    router,
    kc,
    vc,
    pk,
    pv,
    wo,
    wg,
    wu,
    wd,
    qsend,
    qall,
    psend,
    prec,
    asend,
    aall,
    tsend,
    trec,
    xsend,
    xall,
    asend2,
    arecv2,
    ypair,
    yrec,
    zsend,
    zrec,
    hsend,
    hrec,
    sel,
    cntk,
    disp,
    hot128,
    raug,
    gpad,
    hpad,
    hplaced,
    pbs,
    attended,
    hres,
    local_sem,
    down_sem,
    send_sem,
    recv_sem,
):
    r = lax.axis_index("row")
    c = lax.axis_index("col")
    rx, ry, rc = r // (NY * NCORE), (r // NCORE) % NY, r % NCORE

    def row_peer(t):
        dx, dy, dc = t
        return ((rx + dx) % NX) * (NY * NCORE) + ((ry + dy) % NY) * NCORE + (rc + dc) % NCORE

    def col_peer(d):
        return (c + d) % NC

    barrier = pltpu.get_barrier_semaphore()
    for t in ROW_PEERS:
        pl.semaphore_signal(barrier, inc=1, device_id={"row": row_peer(t), "col": c}, device_id_type=pl.DeviceIdType.MESH)
    for d in COL_PEERS:
        pl.semaphore_signal(barrier, inc=1, device_id={"row": r, "col": col_peer(d)}, device_id_type=pl.DeviceIdType.MESH)

    loads = [
        pltpu.make_async_copy(s, t, local_sem.at[i])
        for i, (s, t) in enumerate(
            (
                (queries_h, queries),
                (experts_h, experts_s),
                (cache_keys, kc),
                (cache_values, vc),
                (prefix_keys.at[0], pk),
                (prefix_values.at[0], pv),
                (lengths_h, lengths),
                (new_keys_h, new_keys),
                (new_values_h, new_values),
                (resident_h, resident_s),
                (resident_h, resident),
                (page_table_h, page_table),
                (router_h, router),
                (gain_h, gain),
                (hidden_h, hidden),
                (out_weight, wo),
                (gate_weight.at[0], wg),
                (up_weight.at[0], wu),
            )
        )
    ]
    loads += [
        pltpu.make_async_copy(
            down_weight.at[0, :, pl.ds(pl.multiple_of(2 * WIDTH * k + 128 * rc, 128), WPAD)],
            wd.at[k, pl.ds(pl.multiple_of(rc * FSLICE, FSLICE), FSLICE)],
            down_sem.at[0],
        )
        for k in range(CHIPS)
    ]
    for load in loads:
        load.start()

    def to_row(phase, src_of, dst, only=None):
        for t in ROW_PEERS:
            if only is not None and t[0] != only:
                continue
            peer = row_peer(t)
            pltpu.make_async_remote_copy(
                src_ref=src_of(peer),
                dst_ref=dst.at[r],
                send_sem=send_sem.at[phase],
                recv_sem=recv_sem.at[phase, (NX - t[0]) % NX],
                device_id={"row": peer, "col": c},
                device_id_type=pl.DeviceIdType.MESH,
            ).start()

    def to_chips(phase, src_of, dst, only=None):
        for t in CHIP_PEERS:
            if only is not None and t[0] != only:
                continue
            peer = row_peer(t)
            pltpu.make_async_remote_copy(
                src_ref=src_of(peer // NCORE),
                dst_ref=dst,
                send_sem=send_sem.at[phase],
                recv_sem=recv_sem.at[phase, (NX - t[0]) % NX],
                device_id={"row": peer, "col": c},
                device_id_type=pl.DeviceIdType.MESH,
            ).start()

    def to_partner(phase, src, dst, dx):
        pltpu.make_async_remote_copy(
            src_ref=src,
            dst_ref=dst,
            send_sem=send_sem.at[phase],
            recv_sem=recv_sem.at[phase, dx],
            device_id={"row": row_peer((0, 0, 1)), "col": c},
            device_id_type=pl.DeviceIdType.MESH,
        ).start()

    def chips_of(dx):
        return pl.ds(((rx + dx) % NX) * NY, NY)

    def to_col(phase, src_of, dst):
        for d in COL_PEERS:
            peer = col_peer(d)
            pltpu.make_async_remote_copy(
                src_ref=src_of(peer),
                dst_ref=dst.at[c],
                send_sem=send_sem.at[phase],
                recv_sem=recv_sem.at[phase, 0],
                device_id={"row": r, "col": peer},
                device_id_type=pl.DeviceIdType.MESH,
            ).start()

    def wait_for(sem, buffer, count):
        part = buffer.at[pl.ds(0, count)]
        pltpu.make_async_copy(part, part, sem).wait()

    def first_of(dx):
        return ((rx + dx) % NX) * PER_X

    def group_here(phase, buffer, dx):
        wait_for(recv_sem.at[phase, dx], buffer, PER_X - 1 if dx == 0 else PER_X)

    loads[0].wait()
    loads[1].wait()
    q = queries[...].astype(F32)
    qrows = jnp.concatenate(
        [q[:, g * HD : (g + 1) * HD] for g in range(GROUP)] + [jnp.zeros((HROWS - 2 * GROUP, HD), F32)], axis=0
    )
    q16 = qrows.astype(BF16)
    qsend[...] = q16
    qall[r] = q16
    e_i, b_i = iota((EXPERTS, 128), 0), iota((EXPERTS, 128), 1)
    hot = jnp.zeros((EXPERTS, 128), F32)
    for b in range(BLOCK):
        named = (e_i == experts_s[0, b]) | (e_i == experts_s[1, b])
        hot = jnp.where(named & (b_i == c * BLOCK + b), 1.0, hot)
    hsend[...] = hot
    hrec[c] = hot

    pl.semaphore_wait(barrier, len(ROW_PEERS) + len(COL_PEERS))
    to_row(0, lambda peer: qsend, qall)
    to_col(1, lambda peer: hsend, hrec)

    for k in range(CHIPS):
        pltpu.make_async_remote_copy(
            src_ref=down_weight.at[0, :, pl.ds(pl.multiple_of(2 * WIDTH * k + 128 * (1 - rc), 128), WPAD)],
            dst_ref=wd.at[k, pl.ds(pl.multiple_of(rc * FSLICE, FSLICE), FSLICE)],
            send_sem=down_sem.at[1],
            recv_sem=down_sem.at[2],
            device_id={"row": row_peer((0, 0, 1)), "col": c},
            device_id_type=pl.DeviceIdType.MESH,
        ).start()

    for i in range(9, 15):
        loads[i].wait()
    table = page_table[...]
    res = resident[...]
    flat = iota(res.shape, 1) * SLOTS + iota(res.shape, 0)
    for j in range(SLOTS):
        page = resident_s[j, r]
        earlier = jnp.sum(jnp.where((res == page) & (flat < r * SLOTS + j), 1.0, 0.0), keepdims=True)
        times = jnp.where((table == page) & (earlier == 0.0), 1.0, 0.0)
        cntk[j * PAGE : (j + 1) * PAGE, :] = jnp.broadcast_to(jnp.sum(times, axis=0, keepdims=True), (PAGE, SEQS)).astype(BF16)
    want, have = iota((GROUP * 2 * PER_X, PER_X * HROWS), 0), iota((GROUP * 2 * PER_X, PER_X * HROWS), 1)
    token = want % (2 * PER_X)
    there = (token // 2) * HROWS + 2 * (want // (2 * PER_X)) + token % 2
    sel[...] = jnp.where(have == there, 1.0, 0.0).astype(BF16)
    here = jnp.where(iota((SEQS, BLOCK), 0) == c * BLOCK + iota((SEQS, BLOCK), 1), 1.0, 0.0).astype(BF16)
    place = jnp.where(
        (iota((EXPERTS, WPAD), 1) >= WIDTH) & (iota((EXPERTS, WPAD), 1) < WIDTH + 48)
        & ((iota((EXPERTS, WPAD), 1) - WIDTH) % 16 == iota((EXPERTS, WPAD), 0)), 1.0, 0.0
    ).astype(BF16)
    raug[...] = lax.dot_general(router[...], place, (((0,), (0,)), ((), ())), preferred_element_type=F32).astype(BF16)
    gpad[...] = jnp.zeros_like(gpad)
    gpad[0:1, 0:WIDTH] = gain[...]
    hpad[...] = jnp.zeros_like(hpad)
    hpad[:, 0:WIDTH] = hidden[...].astype(F32)
    hplaced[...] = dot(here, hpad[...].astype(BF16))
    pbs[...] = jnp.zeros_like(pbs)
    hot128[...] = jnp.zeros_like(hot128)

    for i in (2, 6, 7, 8):
        loads[i].wait()
    odd = iota((HROWS, 1), 0) % 2 == 1
    own = [nt_dot(q16, kc[s]) for s in range(2)]
    scores = jnp.where(odd, own[1], own[0]) * SCALE
    length = jnp.where(odd, lengths[1], lengths[0])
    scores = jnp.where(iota((HROWS, CTX), 1) < length, scores, NEG)
    fresh_k = jnp.where(odd, new_keys[1:2, :].astype(F32), new_keys[0:1, :].astype(F32))
    fresh_v = jnp.where(odd, new_values[1:2, :].astype(F32), new_values[0:1, :].astype(F32))
    fresh = jnp.sum(qrows * fresh_k, axis=1, keepdims=True) * SCALE
    peak = jnp.maximum(jnp.max(scores, axis=1, keepdims=True), fresh)
    expo = jnp.exp(scores - peak)
    fresh_e = jnp.exp(fresh - peak)
    own_total = jnp.sum(expo, axis=1, keepdims=True) + fresh_e
    loads[3].wait()
    mixed = (
        dot(jnp.where(odd, 0.0, expo).astype(BF16), vc[0])
        + dot(jnp.where(odd, expo, 0.0).astype(BF16), vc[1])
        + fresh_e.astype(BF16).astype(F32) * fresh_v
    )
    own_peak = peak

    loads[4].wait()
    loads[5].wait()
    n = PER_X * HROWS
    k_i = iota((n, HD), 0) % HROWS
    seq = (iota((n, SEQS), 0) // HROWS) * 2 + iota((n, SEQS), 0) % 2
    for dx in ORDER1:
        group_here(0, qall, dx)
        base = first_of(dx)
        qs = qall[pl.ds(base, PER_X)].reshape(n, HD)
        member = seq + 2 * base == iota((n, SEQS), 1)
        times = nt_dot(jnp.where(member, 1.0, 0.0).astype(BF16), cntk[...])
        sc = nt_dot(qs, pk[...].reshape(KEYS, HD)) * SCALE
        sc = jnp.where(times > 0.0, sc, NEG)
        m = jnp.max(sc, axis=1, keepdims=True)
        e = jnp.exp(sc - m) * times
        l = jnp.sum(e, axis=1, keepdims=True)
        o = dot(e.astype(BF16), pv[...].reshape(KEYS, HD))
        some = l > 0.0
        safe = jnp.where(some, l, 1.0)
        o = o / safe
        lse = jnp.where(some, m + jnp.log(safe), NEG)
        diag = jnp.where(k_i == iota((n, HD), 1), lse, 0.0)
        across = jnp.sum(diag.reshape(PER_X, HROWS, HD), axis=1, keepdims=True)
        across = jnp.broadcast_to(across, (PER_X, HROWS, HD)).reshape(n, HD)
        hi = across.astype(BF16).astype(F32)
        mid = (across - hi).astype(BF16).astype(F32)
        lo = across - hi - mid
        tail = jnp.where(k_i == 12, hi, jnp.where(k_i == 13, mid, jnp.where(k_i == 14, lo, 0.0)))
        psend[pl.ds(base, PER_X)] = jnp.where(k_i < 12, o, tail).astype(BF16).reshape(PER_X, HROWS, HD)
        if dx == 0:
            prec[r] = psend[r]
        to_row(2, lambda peer: psend.at[peer], prec, dx)

    wait_for(recv_sem.at[1, 0], hrec, NC - 1)
    hot = jnp.sum(hrec[...], axis=0)
    hot128[0:EXPERTS, :] = hot
    u0, u1 = iota((128, 128), 0), iota((128, 128), 1)
    before = jnp.where((u0 < u1) & (u0 // BLOCK == u1 // BLOCK), 1.0, 0.0).astype(BF16)
    rank = dot(hot.astype(BF16), before)
    d_r, d_l = iota((ROWS, 128), 0), iota((ROWS, 128), 1)
    for e in range(EXPERTS):
        hit = (
            (hot[e : e + 1, :] > 0.0)
            & (rank[e : e + 1, :] == (d_r % CAP).astype(F32))
            & (d_l // BLOCK == d_r // CAP)
        )
        home = d_l % SEQS == e * BLOCK + d_r % BLOCK
        low = jnp.where(hit & (d_l < SEQS), 1.0, 0.0) + jnp.where(
            home & (d_l >= SEQS) & (d_r // BLOCK == 0), 1.0, 0.0
        )
        high = jnp.where(home & (d_r // BLOCK == 1 + d_l // SEQS), 1.0, 0.0)
        disp[e * ROWS : (e + 1) * ROWS, 0:128] = low.astype(BF16)
        disp[e * ROWS : (e + 1) * ROWS, 128:256] = high.astype(BF16)

    on_diag = iota((PER_X, HROWS, HD), 1) == iota((PER_X, HROWS, HD), 2)
    real = iota((PER_X, HROWS, 1), 1) < 12
    merged = [(own_peak, own_total, mixed)]
    for dx in ORDER2:
        group_here(2, prec, dx)
        parts = prec[pl.ds(first_of(dx), PER_X)].astype(F32)
        lrow = parts[:, 12:13, :] + parts[:, 13:14, :] + parts[:, 14:15, :]
        lse = jnp.sum(jnp.where(on_diag, jnp.broadcast_to(lrow, parts.shape), 0.0), axis=2, keepdims=True)
        lse = jnp.where(real, lse, NEG)
        top = jnp.max(lse, axis=0)
        w = jnp.exp(lse - top[None])
        w = jnp.where(lse > 0.5 * NEG, w, 0.0)
        merged.append((top, jnp.sum(w, axis=0), jnp.sum(w * parts, axis=0)))
    top = functools.reduce(jnp.maximum, [m for m, _, _ in merged])
    ws = [jnp.exp(m - top) for m, _, _ in merged]
    total = sum(w * l for w, (_, l, _) in zip(ws, merged))
    mixed = sum(w * o for w, (_, _, o) in zip(ws, merged))
    att = jnp.where(iota((HROWS, HD), 0) < 12, mixed / total, 0.0).astype(BF16)
    asend[...] = att
    aall[r] = att
    to_row(3, lambda peer: asend, aall)

    loads[15].wait()
    for dx in ORDER3:
        group_here(3, aall, dx)
        base = first_of(dx)
        picked = dot(sel[...], aall[pl.ds(base, PER_X)].reshape(PER_X * HROWS, HD)).astype(BF16)
        tokens = 2 * PER_X
        heads = jnp.concatenate([picked[g * tokens : (g + 1) * tokens] for g in range(GROUP)], axis=1)
        attended[pl.ds(pl.multiple_of(2 * base, tokens), tokens), :] = heads
    pbs[:, 0:WIDTH] = nt_dot(attended[...], wo[...])
    plain = pbs[...]
    with_hidden = plain + hplaced[...]
    lane = iota((SEQS, WPAD), 1)
    moved = [jnp.where(lane >= WIDTH, pltpu.roll(plain, WIDTH - 64 * i, 1), 0.0) for i in range(3)]
    stacked = jnp.concatenate([with_hidden] + moved, axis=0).astype(BF16)
    tsend[...] = dot(disp[...], stacked).astype(BF16).reshape(NC, ROWS, WPAD)
    trec[c] = tsend[c]
    to_col(4, lambda peer: tsend.at[peer], trec)

    wait_for(recv_sem.at[4, 0], trec, NC - 1)
    resid = jnp.sum(trec[...].astype(F32), axis=0)
    lane8 = iota((BLOCK, WPAD), 1)
    home = hpad[...]
    for i in range(3):
        piece = pltpu.roll(resid[i * BLOCK : (i + 1) * BLOCK, :], (64 * i + 64) % WPAD, 1)
        home = home + jnp.where(lane8 // 64 == i, piece, 0.0)
    hres[...] = home
    lane32 = iota((ROWS, WPAD), 1)
    squares = jnp.sum(jnp.where(lane32 < WIDTH, resid * resid, 0.0), axis=1, keepdims=True)
    x = resid * gpad[0:1, :]
    stats = dot(x[:, 0:WIDTH].astype(BF16), raug[...])
    stats = stats + jnp.where((lane32 >= WIDTH) & ((lane32 - WIDTH) % 16 == 8), squares, 0.0)
    hi = stats.astype(BF16).astype(F32)
    mid = (stats - hi).astype(BF16).astype(F32)
    lo = stats - hi - mid
    x = jnp.where(lane32 < WIDTH, x, jnp.where(lane32 < WIDTH + 16, hi, jnp.where(lane32 < WIDTH + 32, mid, jnp.where(lane32 < WIDTH + 48, lo, 0.0))))
    x = jnp.where(rc == 0, x, pltpu.roll(x, 64, 1)).astype(BF16)
    xsend[...] = x
    chip = r // NCORE
    xall[rc, chip] = x
    to_chips(5, lambda peer: xsend, xall.at[rc, chip])

    loads[16].wait()
    loads[17].wait()
    mine = disp[pl.ds(pl.multiple_of(c * ROWS, ROWS), ROWS), 0:128]
    mine = jnp.where(iota((ROWS, 128), 1) < SEQS, mine.astype(F32), 0.0)
    inner_gate = jnp.zeros((ROWS, FSLICE), F32)
    inner_up = jnp.zeros((ROWS, FSLICE), F32)
    even_st = jnp.zeros((ROWS, 128), F32)
    odd_st = jnp.zeros((ROWS, 128), F32)
    low_half = iota((ROWS, 128), 1) < 64
    for dx in ARRIVAL:
        wait_for(recv_sem.at[5, dx], xall.at[rc], NY - 1 if dx == 0 else NY)
        part = xall.at[rc, chips_of(dx)]
        to_partner(8, part, part, dx)
    for dx in ARRIVAL:
        wait_for(recv_sem.at[8, dx], xall.at[rc], NY)
        base = first_of(dx)
        pieces = []
        for j in range(NY):
            even, odd_x = xall[0, base // 2 + j], xall[1, base // 2 + j]
            pieces += [even[:, 0:128], jnp.where(low_half, even[:, 128:256], odd_x[:, 0:128]), odd_x[:, 128:256]]
            even_st = even_st + even[:, 128:256].astype(F32)
            odd_st = odd_st + odd_x[:, 0:128].astype(F32)
        xs = jnp.concatenate(pieces, axis=1)
        rows = pl.ds(pl.multiple_of(base * WIDTH, PER_X * WIDTH), PER_X * WIDTH)
        inner_gate = inner_gate + dot(xs, wg[rows, :])
        inner_up = inner_up + dot(xs, wu[rows, :])
    st = pltpu.roll(even_st, 64, 1) + odd_st
    st = st + pltpu.roll(st, 112, 1) + pltpu.roll(st, 96, 1)
    lane128 = iota((ROWS, 128), 1)
    squares = jnp.sum(jnp.where(lane128 == 8, st, 0.0), axis=1, keepdims=True)
    inverse = lax.rsqrt(squares / D + EPS)
    pair = nt_dot(mine.astype(BF16), hot128[...].astype(BF16))
    logits = st * inverse
    own_logit = jnp.sum(jnp.where(lane128 == c, logits, 0.0), axis=1, keepdims=True)
    other = jnp.sum(jnp.where((pair > 0.0) & (lane128 != c), logits, 0.0), axis=1, keepdims=True)
    share = 1.0 / (1.0 + jnp.exp(other - own_logit))
    inner_gate = inner_gate * inverse
    inner_up = inner_up * inverse
    act = (inner_gate / (1.0 + jnp.exp(-inner_gate)) * inner_up * share).astype(BF16)
    asend2[...] = act
    to_partner(9, asend2, arecv2, 0)
    half = wd.at[:, pl.ds(0, FSLICE)]
    pltpu.make_async_copy(half, half, down_sem.at[0]).wait()
    pltpu.make_async_copy(half, half, down_sem.at[2]).wait()
    pltpu.make_async_copy(arecv2, arecv2, recv_sem.at[9, 0]).wait()
    other = arecv2[...]
    act = jnp.concatenate([jnp.where(rc == 0, act, other), jnp.where(rc == 0, other, act)], axis=1)
    for dx in FAR_FIRST:
        base = ((rx + dx) % NX) * NY
        for j in range(NY):
            ypair[base + j] = dot(act, wd[base + j]).astype(BF16)
        if dx == 0:
            yrec[chip] = ypair[chip]
        to_chips(6, lambda peer: ypair.at[peer], yrec.at[chip], dx)

    ysum = jnp.zeros((ROWS, WPAD), F32)
    for dx in NEAR_FIRST:
        wait_for(recv_sem.at[6, dx], yrec, NY - 1 if dx == 0 else NY)
        ysum = ysum + jnp.sum(yrec[chips_of(dx)].astype(F32), axis=0)
    ysum = jnp.where(rc == 0, ysum, pltpu.roll(ysum, WPAD - 64, 1))
    back = lax.dot_general(
        mine.astype(BF16), ysum.astype(BF16), (((0,), (0,)), ((), ())), preferred_element_type=F32
    )
    for i in range(NC):
        both = jnp.concatenate(
            [back[i * BLOCK : (i + 1) * BLOCK, 0:128], back[i * BLOCK : (i + 1) * BLOCK, 128:256]], axis=0
        )
        zsend[i] = both.astype(BF16)
    zrec[c] = zsend[c]
    to_col(7, lambda peer: zsend.at[peer], zrec)
    wait_for(recv_sem.at[7, 0], zrec, NC - 1)
    z = jnp.sum(zrec[...].astype(F32), axis=0)
    final = hres[...]
    out[:, 0:128] = (final[:, 0:128] + z[0:BLOCK]).astype(out.dtype)
    out[:, 128:WIDTH] = (final[:, 128:WIDTH] + z[BLOCK:, 0 : WIDTH - 128]).astype(out.dtype)

    wait_for(send_sem.at[0], qall, NR - 1)
    wait_for(send_sem.at[1], hrec, NC - 1)
    wait_for(send_sem.at[2], prec, NR - 1)
    wait_for(send_sem.at[3], aall, NR - 1)
    wait_for(send_sem.at[4], trec, NC - 1)
    wait_for(send_sem.at[5], yrec, CHIPS - 1)
    wait_for(send_sem.at[6], yrec, CHIPS - 1)
    wait_for(send_sem.at[8], yrec, CHIPS)
    pltpu.make_async_copy(arecv2, arecv2, send_sem.at[9]).wait()
    pltpu.make_async_copy(half, half, down_sem.at[1]).wait()
    wait_for(send_sem.at[7], zrec, NC - 1)


def body(
    hidden,
    queries,
    new_keys,
    new_values,
    cache_keys,
    cache_values,
    lengths,
    page_table,
    resident,
    prefix_keys,
    prefix_values,
    out_weight,
    norm_gain,
    router_weight,
    experts,
    gate_weight,
    up_weight,
    down_projection_weight,
):
    hbm = pl.BlockSpec(memory_space=pltpu.HBM)
    vmem = pl.BlockSpec(memory_space=pltpu.VMEM)
    return pl.pallas_call(
        kernel,
        out_shape=jax.ShapeDtypeStruct((BLOCK, WIDTH), BF16),
        in_specs=[hbm] * 18,
        out_specs=vmem,
        scratch_shapes=[
            pltpu.SMEM((2,), jnp.int32),
            pltpu.SMEM((SLOTS, NR), jnp.int32),
            pltpu.SMEM((2, BLOCK), jnp.int32),
            pltpu.VMEM((BLOCK, WIDTH), BF16),
            pltpu.VMEM((2, GROUP * HD), BF16),
            pltpu.VMEM((2, HD), BF16),
            pltpu.VMEM((2, HD), BF16),
            pltpu.VMEM((8, SEQS), jnp.int32),
            pltpu.VMEM((SLOTS, NR), jnp.int32),
            pltpu.VMEM((1, WIDTH), F32),
            pltpu.VMEM((EXPERTS, WIDTH), BF16),
            pltpu.VMEM((2, CTX, HD), BF16),
            pltpu.VMEM((2, CTX, HD), BF16),
            pltpu.VMEM((SLOTS, PAGE, HD), BF16),
            pltpu.VMEM((SLOTS, PAGE, HD), BF16),
            pltpu.VMEM((WIDTH, GROUP * HD), BF16),
            pltpu.VMEM((D, FSLICE), BF16),
            pltpu.VMEM((D, FSLICE), BF16),
            pltpu.VMEM((CHIPS, NCORE * FSLICE, WPAD), BF16),
            pltpu.VMEM((HROWS, HD), BF16),
            pltpu.VMEM((NR, HROWS, HD), BF16),
            pltpu.VMEM((NR, HROWS, HD), BF16),
            pltpu.VMEM((NR, HROWS, HD), BF16),
            pltpu.VMEM((HROWS, HD), BF16),
            pltpu.VMEM((NR, HROWS, HD), BF16),
            pltpu.VMEM((NC, ROWS, WPAD), BF16),
            pltpu.VMEM((NC, ROWS, WPAD), BF16),
            pltpu.VMEM((ROWS, WPAD), BF16),
            pltpu.VMEM((NCORE, CHIPS, ROWS, WPAD), BF16),
            pltpu.VMEM((ROWS, FSLICE), BF16),
            pltpu.VMEM((ROWS, FSLICE), BF16),
            pltpu.VMEM((CHIPS, ROWS, WPAD), BF16),
            pltpu.VMEM((CHIPS, ROWS, WPAD), BF16),
            pltpu.VMEM((NC, 2 * BLOCK, 128), BF16),
            pltpu.VMEM((NC, 2 * BLOCK, 128), BF16),
            pltpu.VMEM((EXPERTS, 128), F32),
            pltpu.VMEM((NC, EXPERTS, 128), F32),
            pltpu.VMEM((GROUP * 2 * PER_X, PER_X * HROWS), BF16),
            pltpu.VMEM((KEYS, SEQS), BF16),
            pltpu.VMEM((NC * ROWS, WPAD), BF16),
            pltpu.VMEM((128, 128), F32),
            pltpu.VMEM((WIDTH, WPAD), BF16),
            pltpu.VMEM((8, WPAD), F32),
            pltpu.VMEM((BLOCK, WPAD), F32),
            pltpu.VMEM((SEQS, WPAD), F32),
            pltpu.VMEM((SEQS, WPAD), F32),
            pltpu.VMEM((SEQS, GROUP * HD), BF16),
            pltpu.VMEM((BLOCK, WPAD), F32),
            pltpu.SemaphoreType.DMA((18,)),
            pltpu.SemaphoreType.DMA((3,)),
            pltpu.SemaphoreType.DMA((10,)),
            pltpu.SemaphoreType.DMA((10, NX)),
        ],
        compiler_params=pltpu.CompilerParams(
            collective_id=0, has_side_effects=True, vmem_limit_bytes=67043328
        ),
        name="layer",
    )(
        lengths,
        resident.T,
        experts.T,
        hidden,
        queries,
        new_keys,
        new_values,
        page_table.T,
        norm_gain.reshape(1, WIDTH),
        router_weight.T,
        cache_keys,
        cache_values,
        prefix_keys,
        prefix_values,
        out_weight.T,
        gate_weight,
        up_weight,
        down_projection_weight,
    )


def solution(mesh):
    in_specs = (
        P("col", "row"),
        P("row", "col"),
        P("row", "col"),
        P("row", "col"),
        P("row", None, "col"),
        P("row", None, "col"),
        P("row"),
        P(),
        P(),
        P("row", None, None, "col"),
        P("row", None, None, "col"),
        P("col", "row"),
        P("row"),
        P("row", None),
        P("col", None),
        P("col", None, "row"),
        P("col", None, "row"),
        P("col", "row", None),
    )
    return jax.shard_map(body, mesh=mesh, in_specs=in_specs, out_specs=P("col", "row"), check_vma=False)
```

time: 74.3 us -> 53 us (0.71)
  local copies, waits for them, and re-layouts: 15 us -> 1.28 us
  Pallas kernels: 58.8 us -> 51.2 us
    unnamed x28 -> x1, local copies, waits for them, and re-layouts: 15 us -> 1.28 us
    pallas_call x1, Pallas kernels: 58.8 us -> 51.2 us  [body(): pl.pallas_call(kernel, out_shape=jax.ShapeDtypeStruct((BLOCK, WIDTH), BF1...]
where the time goes in v2:
time: 53 us; the launch traced here: 52.5 us
  Pallas kernels  51.2 us (97%)
  local copies, waits for them, and re-layouts  1.28 us (2%)
    pallas_call x1, Pallas kernels, body(): pl.pallas_call(kernel, out_shape=jax.ShapeDtypeStruct((BLOCK, WIDTH), BF1...  51.2 us
    unnamed x1, local copies, waits for them, and re-layouts  1.28 us

profile of v2, /device:TPU:1, one launch (start us, length us, event | category | flops | bytes accessed | tf_op | source)
XLA Modules:
  0.0 52.5 jit_solution(6116294261904670709)
XLA Ops:
  0.0 51.2 %layer.1 = bf16[8,192]{1,0:T(8,128)(2,1)} custom-call(s32[2]{0:T(128)} %lengths_h.1, s32[4,32]{1,0:T(4,128)} %bitcast.9, s32[2,8]{1,0:T(2,128)} %bitcast.10, bf16[8,192]{1,0:T(8,128)(2,1)} %hidden_h.1, bf16[2,768]{1,0:T(2,128)(2,1)} %queries_h.1, bf16[2,128]{1,0:T(2,128)(2,1)} %new_keys_h.1, bf16[2,128]{1,0:T(2,128)(2,1)} %new_values_h.1, s32[8,64]{1,0:T(8,128)} %bitcast.7, ...), custom_call_target="tpu_custom_call" | custom-call | tf_op jit(solution)/shard_map/layer/pallas_call | solution.py:568
  51.2 1.3 %copy.20 = bf16[8,192]{1,0:T(8,128)(2,1)} copy(bf16[8,192]{1,0:T(8,128)(2,1)} %layer.1) | data formatting | bytes 6144

commit v3 on v2

--- a/solution.py
+++ b/solution.py
@@ -44,6 +44,8 @@
 ]
 ROW_PEERS.sort(key=lambda t: -(min(t[0], NX - t[0]) + min(t[1], NY - t[1]) + 0.5 * t[2]))
 PER_X = NY * NCORE
+RECV = (0, 20, 4, 21, 22, 8, 16, 23, 12, 24)
+LOCAL = (0, 1, 2, 2, 3, 3, 4, 5, 5, 6, 7, 8, 9, 10, 11, 12, 13, 13)
 NEAR_FIRST = (0, 1, 3, 2)
 ARRIVAL = (2, 1, 3, 0)
 ORDER1 = (0, 1, 3, 2)
@@ -92,19 +94,15 @@
     experts_s,
     hidden,
     queries,
-    new_keys,
-    new_values,
+    fresh_kv,
     page_table,
     resident,
     gain,
     router,
-    kc,
-    vc,
-    pk,
-    pv,
+    kv,
+    pkv,
     wo,
-    wg,
-    wu,
+    wgu,
     wd,
     qsend,
     qall,
@@ -158,18 +156,18 @@
         pl.semaphore_signal(barrier, inc=1, device_id={"row": r, "col": col_peer(d)}, device_id_type=pl.DeviceIdType.MESH)
 
     loads = [
-        pltpu.make_async_copy(s, t, local_sem.at[i])
+        pltpu.make_async_copy(s, t, local_sem.at[LOCAL[i]])
         for i, (s, t) in enumerate(
             (
                 (queries_h, queries),
                 (experts_h, experts_s),
-                (cache_keys, kc),
-                (cache_values, vc),
-                (prefix_keys.at[0], pk),
-                (prefix_values.at[0], pv),
+                (cache_keys, kv.at[0]),
+                (cache_values, kv.at[1]),
+                (prefix_keys.at[0], pkv.at[0]),
+                (prefix_values.at[0], pkv.at[1]),
                 (lengths_h, lengths),
-                (new_keys_h, new_keys),
-                (new_values_h, new_values),
+                (new_keys_h, fresh_kv.at[0]),
+                (new_values_h, fresh_kv.at[1]),
                 (resident_h, resident_s),
                 (resident_h, resident),
                 (page_table_h, page_table),
@@ -177,8 +175,8 @@
                 (gain_h, gain),
                 (hidden_h, hidden),
                 (out_weight, wo),
-                (gate_weight.at[0], wg),
-                (up_weight.at[0], wu),
+                (gate_weight.at[0], wgu.at[0]),
+                (up_weight.at[0], wgu.at[1]),
             )
         )
     ]
@@ -202,7 +200,7 @@
                 src_ref=src_of(peer),
                 dst_ref=dst.at[r],
                 send_sem=send_sem.at[phase],
-                recv_sem=recv_sem.at[phase, (NX - t[0]) % NX],
+                recv_sem=recv_sem.at[RECV[phase] + (0 if phase == 3 else (NX - t[0]) % NX)],
                 device_id={"row": peer, "col": c},
                 device_id_type=pl.DeviceIdType.MESH,
             ).start()
@@ -216,7 +214,7 @@
                 src_ref=src_of(peer // NCORE),
                 dst_ref=dst,
                 send_sem=send_sem.at[phase],
-                recv_sem=recv_sem.at[phase, (NX - t[0]) % NX],
+                recv_sem=recv_sem.at[RECV[phase] + (0 if phase == 3 else (NX - t[0]) % NX)],
                 device_id={"row": peer, "col": c},
                 device_id_type=pl.DeviceIdType.MESH,
             ).start()
@@ -226,7 +224,7 @@
             src_ref=src,
             dst_ref=dst,
             send_sem=send_sem.at[phase],
-            recv_sem=recv_sem.at[phase, dx],
+            recv_sem=recv_sem.at[RECV[phase] + dx],
             device_id={"row": row_peer((0, 0, 1)), "col": c},
             device_id_type=pl.DeviceIdType.MESH,
         ).start()
@@ -241,7 +239,7 @@
                 src_ref=src_of(peer),
                 dst_ref=dst.at[c],
                 send_sem=send_sem.at[phase],
-                recv_sem=recv_sem.at[phase, 0],
+                recv_sem=recv_sem.at[RECV[phase]],
                 device_id={"row": r, "col": peer},
                 device_id_type=pl.DeviceIdType.MESH,
             ).start()
@@ -250,11 +248,14 @@
         part = buffer.at[pl.ds(0, count)]
         pltpu.make_async_copy(part, part, sem).wait()
 
+    def both_here(i, buffer):
+        pltpu.make_async_copy(buffer, buffer, local_sem.at[i]).wait()
+
     def first_of(dx):
         return ((rx + dx) % NX) * PER_X
 
     def group_here(phase, buffer, dx):
-        wait_for(recv_sem.at[phase, dx], buffer, PER_X - 1 if dx == 0 else PER_X)
+        wait_for(recv_sem.at[RECV[phase] + dx], buffer, PER_X - 1 if dx == 0 else PER_X)
 
     loads[0].wait()
     loads[1].wait()
@@ -315,30 +316,29 @@
     pbs[...] = jnp.zeros_like(pbs)
     hot128[...] = jnp.zeros_like(hot128)
 
-    for i in (2, 6, 7, 8):
-        loads[i].wait()
+    loads[6].wait()
+    both_here(5, fresh_kv)
+    both_here(2, kv)
     odd = iota((HROWS, 1), 0) % 2 == 1
-    own = [nt_dot(q16, kc[s]) for s in range(2)]
+    own = [nt_dot(q16, kv[0, s]) for s in range(2)]
     scores = jnp.where(odd, own[1], own[0]) * SCALE
     length = jnp.where(odd, lengths[1], lengths[0])
     scores = jnp.where(iota((HROWS, CTX), 1) < length, scores, NEG)
-    fresh_k = jnp.where(odd, new_keys[1:2, :].astype(F32), new_keys[0:1, :].astype(F32))
-    fresh_v = jnp.where(odd, new_values[1:2, :].astype(F32), new_values[0:1, :].astype(F32))
+    fresh_k = jnp.where(odd, fresh_kv[0, 1:2, :].astype(F32), fresh_kv[0, 0:1, :].astype(F32))
+    fresh_v = jnp.where(odd, fresh_kv[1, 1:2, :].astype(F32), fresh_kv[1, 0:1, :].astype(F32))
     fresh = jnp.sum(qrows * fresh_k, axis=1, keepdims=True) * SCALE
     peak = jnp.maximum(jnp.max(scores, axis=1, keepdims=True), fresh)
     expo = jnp.exp(scores - peak)
     fresh_e = jnp.exp(fresh - peak)
     own_total = jnp.sum(expo, axis=1, keepdims=True) + fresh_e
-    loads[3].wait()
     mixed = (
-        dot(jnp.where(odd, 0.0, expo).astype(BF16), vc[0])
-        + dot(jnp.where(odd, expo, 0.0).astype(BF16), vc[1])
+        dot(jnp.where(odd, 0.0, expo).astype(BF16), kv[1, 0])
+        + dot(jnp.where(odd, expo, 0.0).astype(BF16), kv[1, 1])
         + fresh_e.astype(BF16).astype(F32) * fresh_v
     )
     own_peak = peak
 
-    loads[4].wait()
-    loads[5].wait()
+    both_here(3, pkv)
     n = PER_X * HROWS
     k_i = iota((n, HD), 0) % HROWS
     seq = (iota((n, SEQS), 0) // HROWS) * 2 + iota((n, SEQS), 0) % 2
@@ -348,12 +348,12 @@
         qs = qall[pl.ds(base, PER_X)].reshape(n, HD)
         member = seq + 2 * base == iota((n, SEQS), 1)
         times = nt_dot(jnp.where(member, 1.0, 0.0).astype(BF16), cntk[...])
-        sc = nt_dot(qs, pk[...].reshape(KEYS, HD)) * SCALE
+        sc = nt_dot(qs, pkv[0].reshape(KEYS, HD)) * SCALE
         sc = jnp.where(times > 0.0, sc, NEG)
         m = jnp.max(sc, axis=1, keepdims=True)
         e = jnp.exp(sc - m) * times
         l = jnp.sum(e, axis=1, keepdims=True)
-        o = dot(e.astype(BF16), pv[...].reshape(KEYS, HD))
+        o = dot(e.astype(BF16), pkv[1].reshape(KEYS, HD))
         some = l > 0.0
         safe = jnp.where(some, l, 1.0)
         o = o / safe
@@ -370,7 +370,7 @@
             prec[r] = psend[r]
         to_row(2, lambda peer: psend.at[peer], prec, dx)
 
-    wait_for(recv_sem.at[1, 0], hrec, NC - 1)
+    wait_for(recv_sem.at[RECV[1]], hrec, NC - 1)
     hot = jnp.sum(hrec[...], axis=0)
     hot128[0:EXPERTS, :] = hot
     u0, u1 = iota((128, 128), 0), iota((128, 128), 1)
@@ -414,9 +414,9 @@
     to_row(3, lambda peer: asend, aall)
 
     loads[15].wait()
-    for dx in ORDER3:
-        group_here(3, aall, dx)
-        base = first_of(dx)
+    wait_for(recv_sem.at[RECV[3]], aall, NR - 1)
+    for dx in range(NX):
+        base = dx * PER_X
         picked = dot(sel[...], aall[pl.ds(base, PER_X)].reshape(PER_X * HROWS, HD)).astype(BF16)
         tokens = 2 * PER_X
         heads = jnp.concatenate([picked[g * tokens : (g + 1) * tokens] for g in range(GROUP)], axis=1)
@@ -431,7 +431,7 @@
     trec[c] = tsend[c]
     to_col(4, lambda peer: tsend.at[peer], trec)
 
-    wait_for(recv_sem.at[4, 0], trec, NC - 1)
+    wait_for(recv_sem.at[RECV[4]], trec, NC - 1)
     resid = jnp.sum(trec[...].astype(F32), axis=0)
     lane8 = iota((BLOCK, WPAD), 1)
     home = hpad[...]
@@ -454,8 +454,7 @@
     xall[rc, chip] = x
     to_chips(5, lambda peer: xsend, xall.at[rc, chip])
 
-    loads[16].wait()
-    loads[17].wait()
+    both_here(13, wgu)
     mine = disp[pl.ds(pl.multiple_of(c * ROWS, ROWS), ROWS), 0:128]
     mine = jnp.where(iota((ROWS, 128), 1) < SEQS, mine.astype(F32), 0.0)
     inner_gate = jnp.zeros((ROWS, FSLICE), F32)
@@ -464,11 +463,11 @@
     odd_st = jnp.zeros((ROWS, 128), F32)
     low_half = iota((ROWS, 128), 1) < 64
     for dx in ARRIVAL:
-        wait_for(recv_sem.at[5, dx], xall.at[rc], NY - 1 if dx == 0 else NY)
+        wait_for(recv_sem.at[RECV[5] + dx], xall.at[rc], NY - 1 if dx == 0 else NY)
         part = xall.at[rc, chips_of(dx)]
         to_partner(8, part, part, dx)
     for dx in ARRIVAL:
-        wait_for(recv_sem.at[8, dx], xall.at[rc], NY)
+        wait_for(recv_sem.at[RECV[8] + dx], xall.at[rc], NY)
         base = first_of(dx)
         pieces = []
         for j in range(NY):
@@ -478,8 +477,8 @@
             odd_st = odd_st + odd_x[:, 0:128].astype(F32)
         xs = jnp.concatenate(pieces, axis=1)
         rows = pl.ds(pl.multiple_of(base * WIDTH, PER_X * WIDTH), PER_X * WIDTH)
-        inner_gate = inner_gate + dot(xs, wg[rows, :])
-        inner_up = inner_up + dot(xs, wu[rows, :])
+        inner_gate = inner_gate + dot(xs, wgu[0, rows, :])
+        inner_up = inner_up + dot(xs, wgu[1, rows, :])
     st = pltpu.roll(even_st, 64, 1) + odd_st
     st = st + pltpu.roll(st, 112, 1) + pltpu.roll(st, 96, 1)
     lane128 = iota((ROWS, 128), 1)
@@ -498,7 +497,7 @@
     half = wd.at[:, pl.ds(0, FSLICE)]
     pltpu.make_async_copy(half, half, down_sem.at[0]).wait()
     pltpu.make_async_copy(half, half, down_sem.at[2]).wait()
-    pltpu.make_async_copy(arecv2, arecv2, recv_sem.at[9, 0]).wait()
+    pltpu.make_async_copy(arecv2, arecv2, recv_sem.at[RECV[9]]).wait()
     other = arecv2[...]
     act = jnp.concatenate([jnp.where(rc == 0, act, other), jnp.where(rc == 0, other, act)], axis=1)
     for dx in FAR_FIRST:
@@ -511,7 +510,7 @@
 
     ysum = jnp.zeros((ROWS, WPAD), F32)
     for dx in NEAR_FIRST:
-        wait_for(recv_sem.at[6, dx], yrec, NY - 1 if dx == 0 else NY)
+        wait_for(recv_sem.at[RECV[6] + dx], yrec, NY - 1 if dx == 0 else NY)
         ysum = ysum + jnp.sum(yrec[chips_of(dx)].astype(F32), axis=0)
     ysum = jnp.where(rc == 0, ysum, pltpu.roll(ysum, WPAD - 64, 1))
     back = lax.dot_general(
@@ -524,7 +523,7 @@
         zsend[i] = both.astype(BF16)
     zrec[c] = zsend[c]
     to_col(7, lambda peer: zsend.at[peer], zrec)
-    wait_for(recv_sem.at[7, 0], zrec, NC - 1)
+    wait_for(recv_sem.at[RECV[7]], zrec, NC - 1)
     z = jnp.sum(zrec[...].astype(F32), axis=0)
     final = hres[...]
     out[:, 0:128] = (final[:, 0:128] + z[0:BLOCK]).astype(out.dtype)
@@ -565,6 +564,26 @@
 ):
     hbm = pl.BlockSpec(memory_space=pltpu.HBM)
     vmem = pl.BlockSpec(memory_space=pltpu.VMEM)
+    operands = (
+        lengths,
+        resident.T,
+        experts.T,
+        hidden,
+        queries,
+        new_keys,
+        new_values,
+        page_table.T,
+        norm_gain.reshape(1, WIDTH),
+        router_weight.T,
+        cache_keys,
+        cache_values,
+        prefix_keys,
+        prefix_values,
+        out_weight.T,
+        gate_weight,
+        up_weight,
+        down_projection_weight,
+    )
     return pl.pallas_call(
         kernel,
         out_shape=jax.ShapeDtypeStruct((BLOCK, WIDTH), BF16),
@@ -576,19 +595,15 @@
             pltpu.SMEM((2, BLOCK), jnp.int32),
             pltpu.VMEM((BLOCK, WIDTH), BF16),
             pltpu.VMEM((2, GROUP * HD), BF16),
-            pltpu.VMEM((2, HD), BF16),
-            pltpu.VMEM((2, HD), BF16),
+            pltpu.VMEM((2, 2, HD), BF16),
             pltpu.VMEM((8, SEQS), jnp.int32),
             pltpu.VMEM((SLOTS, NR), jnp.int32),
             pltpu.VMEM((1, WIDTH), F32),
             pltpu.VMEM((EXPERTS, WIDTH), BF16),
-            pltpu.VMEM((2, CTX, HD), BF16),
-            pltpu.VMEM((2, CTX, HD), BF16),
-            pltpu.VMEM((SLOTS, PAGE, HD), BF16),
-            pltpu.VMEM((SLOTS, PAGE, HD), BF16),
+            pltpu.VMEM((2, 2, CTX, HD), BF16),
+            pltpu.VMEM((2, SLOTS, PAGE, HD), BF16),
             pltpu.VMEM((WIDTH, GROUP * HD), BF16),
-            pltpu.VMEM((D, FSLICE), BF16),
-            pltpu.VMEM((D, FSLICE), BF16),
+            pltpu.VMEM((2, D, FSLICE), BF16),
             pltpu.VMEM((CHIPS, NCORE * FSLICE, WPAD), BF16),
             pltpu.VMEM((HROWS, HD), BF16),
             pltpu.VMEM((NR, HROWS, HD), BF16),
@@ -619,35 +634,16 @@
             pltpu.VMEM((SEQS, WPAD), F32),
             pltpu.VMEM((SEQS, GROUP * HD), BF16),
             pltpu.VMEM((BLOCK, WPAD), F32),
-            pltpu.SemaphoreType.DMA((18,)),
+            pltpu.SemaphoreType.DMA((14,)),
             pltpu.SemaphoreType.DMA((3,)),
             pltpu.SemaphoreType.DMA((10,)),
-            pltpu.SemaphoreType.DMA((10, NX)),
+            pltpu.SemaphoreType.DMA((25,)),
         ],
         compiler_params=pltpu.CompilerParams(
-            collective_id=0, has_side_effects=True, vmem_limit_bytes=67043328
+            collective_id=0, has_side_effects=True, vmem_limit_bytes=40 * 1024 * 1024
         ),
         name="layer",
-    )(
-        lengths,
-        resident.T,
-        experts.T,
-        hidden,
-        queries,
-        new_keys,
-        new_values,
-        page_table.T,
-        norm_gain.reshape(1, WIDTH),
-        router_weight.T,
-        cache_keys,
-        cache_values,
-        prefix_keys,
-        prefix_values,
-        out_weight.T,
-        gate_weight,
-        up_weight,
-        down_projection_weight,
-    )
+    )(*[pltpu.with_memory_space_constraint(a, pltpu.HBM) for a in operands])
 
 
 def solution(mesh):

time: 53 us -> 51.2 us (0.966)
  Pallas kernels: 51.2 us -> 50 us
  local copies, waits for them, and re-layouts: 1.28 us -> 0.6 us
    pallas_call x1, Pallas kernels: 51.2 us -> 50 us  [body(): pl.pallas_call(kernel, out_shape=jax.ShapeDtypeStruct((BLOCK, WIDTH), BF1...]
    unnamed x1, local copies, waits for them, and re-layouts: 1.28 us -> 0.6 us
where the time goes in v3:
time: 51.2 us; the launch traced here: 50.6 us
  Pallas kernels  50 us (98%)
  local copies, waits for them, and re-layouts  0.6 us (1%)
    pallas_call x1, Pallas kernels, body(): pl.pallas_call(kernel, out_shape=jax.ShapeDtypeStruct((BLOCK, WIDTH), BF1...  50 us

profile of v3, /device:TPU:1, one launch (start us, length us, event | category | flops | bytes accessed | tf_op | source)
XLA Modules:
  0.0 50.6 jit_solution(16113318401073204722)
XLA Ops:
  0.0 50.0 %layer.1 = bf16[8,192]{1,0:T(8,128)(2,1)S(1)} custom-call(s32[2]{0:T(128)} %lengths_h.1, s32[4,32]{1,0:T(4,128)} %bitcast.9, s32[2,8]{1,0:T(2,128)} %bitcast.10, bf16[8,192]{1,0:T(8,128)(2,1)} %hidden_h.1, bf16[2,768]{1,0:T(2,128)(2,1)} %queries_h.1, bf16[2,128]{1,0:T(2,128)(2,1)} %new_keys_h.1, bf16[2,128]{1,0:T(2,128)(2,1)} %new_values_h.1, ...), custom_call_target="tpu_custom_call" | custom-call | tf_op jit(solution)/shard_map/layer/pallas_call | solution.py:587
  50.0 0.6 %copy.20 = bf16[8,192]{1,0:T(8,128)(2,1)} copy(bf16[8,192]{1,0:T(8,128)(2,1)S(1)} %layer.1) | data formatting | bytes 6144

commit v4 on v3

--- a/solution.py
+++ b/solution.py
@@ -45,7 +45,7 @@
 ROW_PEERS.sort(key=lambda t: -(min(t[0], NX - t[0]) + min(t[1], NY - t[1]) + 0.5 * t[2]))
 PER_X = NY * NCORE
 RECV = (0, 20, 4, 21, 22, 8, 16, 23, 12, 24)
-LOCAL = (0, 1, 2, 2, 3, 3, 4, 5, 5, 6, 7, 8, 9, 10, 11, 12, 13, 13)
+LOCAL = (0, 1, 2, 2, 3, 3, 4, 5, 5, 6, 7, 8, 9, 10, 11, 12)
 NEAR_FIRST = (0, 1, 3, 2)
 ARRIVAL = (2, 1, 3, 0)
 ORDER1 = (0, 1, 3, 2)
@@ -102,7 +102,7 @@
     kv,
     pkv,
     wo,
-    wgu,
+    wx,
     wd,
     qsend,
     qall,
@@ -114,8 +114,10 @@
     trec,
     xsend,
     xall,
-    asend2,
-    arecv2,
+    insend,
+    inrecv,
+    stsend,
+    strecv,
     ypair,
     yrec,
     zsend,
@@ -175,21 +177,28 @@
                 (gain_h, gain),
                 (hidden_h, hidden),
                 (out_weight, wo),
-                (gate_weight.at[0], wgu.at[0]),
-                (up_weight.at[0], wgu.at[1]),
             )
         )
     ]
     loads += [
         pltpu.make_async_copy(
             down_weight.at[0, :, pl.ds(pl.multiple_of(2 * WIDTH * k + 128 * rc, 128), WPAD)],
-            wd.at[k, pl.ds(pl.multiple_of(rc * FSLICE, FSLICE), FSLICE)],
+            wd.at[pl.ds(0, FSLICE), pl.ds(k * WPAD, WPAD)],
             down_sem.at[0],
         )
         for k in range(CHIPS)
     ]
-    for load in loads:
-        load.start()
+    loads += [
+        pltpu.make_async_copy(
+            w.at[0, pl.ds(pl.multiple_of(2 * WIDTH * k + WIDTH * rc, 64), WIDTH), :],
+            wx.at[pl.ds(k * WIDTH, WIDTH), pl.ds(2 * i * FSLICE, FSLICE)],
+            down_sem.at[3],
+        )
+        for k in range(CHIPS)
+        for i, w in enumerate((gate_weight, up_weight))
+    ]
+    loads[0].start()
+    loads[1].start()
 
     def to_row(phase, src_of, dst, only=None):
         for t in ROW_PEERS:
@@ -259,6 +268,8 @@
 
     loads[0].wait()
     loads[1].wait()
+    for load in loads[2:16]:
+        load.start()
     q = queries[...].astype(F32)
     qrows = jnp.concatenate(
         [q[:, g * HD : (g + 1) * HD] for g in range(GROUP)] + [jnp.zeros((HROWS - 2 * GROUP, HD), F32)], axis=0
@@ -278,10 +289,22 @@
     to_row(0, lambda peer: qsend, qall)
     to_col(1, lambda peer: hsend, hrec)
 
+    for load in loads[16:]:
+        load.start()
+    for k in range(CHIPS):
+        for i, w in enumerate((gate_weight, up_weight)):
+            pltpu.make_async_remote_copy(
+                src_ref=w.at[0, pl.ds(pl.multiple_of(2 * WIDTH * k + WIDTH * (1 - rc), 64), WIDTH), :],
+                dst_ref=wx.at[pl.ds(k * WIDTH, WIDTH), pl.ds((2 * i + 1) * FSLICE, FSLICE)],
+                send_sem=down_sem.at[4],
+                recv_sem=down_sem.at[5],
+                device_id={"row": row_peer((0, 0, 1)), "col": c},
+                device_id_type=pl.DeviceIdType.MESH,
+            ).start()
     for k in range(CHIPS):
         pltpu.make_async_remote_copy(
             src_ref=down_weight.at[0, :, pl.ds(pl.multiple_of(2 * WIDTH * k + 128 * (1 - rc), 128), WPAD)],
-            dst_ref=wd.at[k, pl.ds(pl.multiple_of(rc * FSLICE, FSLICE), FSLICE)],
+            dst_ref=wd.at[pl.ds(FSLICE, FSLICE), pl.ds(k * WPAD, WPAD)],
             send_sem=down_sem.at[1],
             recv_sem=down_sem.at[2],
             device_id={"row": row_peer((0, 0, 1)), "col": c},
@@ -448,38 +471,39 @@
     mid = (stats - hi).astype(BF16).astype(F32)
     lo = stats - hi - mid
     x = jnp.where(lane32 < WIDTH, x, jnp.where(lane32 < WIDTH + 16, hi, jnp.where(lane32 < WIDTH + 32, mid, jnp.where(lane32 < WIDTH + 48, lo, 0.0))))
-    x = jnp.where(rc == 0, x, pltpu.roll(x, 64, 1)).astype(BF16)
+    x = jnp.where(ry % 2 == 0, x, pltpu.roll(x, 64, 1)).astype(BF16)
     xsend[...] = x
     chip = r // NCORE
-    xall[rc, chip] = x
-    to_chips(5, lambda peer: xsend, xall.at[rc, chip])
-
-    both_here(13, wgu)
+    xall[chip] = x
+    to_chips(5, lambda peer: xsend, xall.at[chip])
+
+    half_x = wx.at[pl.ds(0, D // NCORE // 2)]
+    pltpu.make_async_copy(half_x, half_x, down_sem.at[3]).wait()
+    pltpu.make_async_copy(half_x, half_x, down_sem.at[5]).wait()
     mine = disp[pl.ds(pl.multiple_of(c * ROWS, ROWS), ROWS), 0:128]
     mine = jnp.where(iota((ROWS, 128), 1) < SEQS, mine.astype(F32), 0.0)
-    inner_gate = jnp.zeros((ROWS, FSLICE), F32)
-    inner_up = jnp.zeros((ROWS, FSLICE), F32)
+    inner = jnp.zeros((ROWS, 4 * FSLICE), F32)
     even_st = jnp.zeros((ROWS, 128), F32)
     odd_st = jnp.zeros((ROWS, 128), F32)
     low_half = iota((ROWS, 128), 1) < 64
-    for dx in ARRIVAL:
-        wait_for(recv_sem.at[RECV[5] + dx], xall.at[rc], NY - 1 if dx == 0 else NY)
-        part = xall.at[rc, chips_of(dx)]
-        to_partner(8, part, part, dx)
-    for dx in ARRIVAL:
-        wait_for(recv_sem.at[RECV[8] + dx], xall.at[rc], NY)
-        base = first_of(dx)
+    for dx in NEAR_FIRST:
+        wait_for(recv_sem.at[RECV[5] + dx], xall, NY - 1 if dx == 0 else NY)
+        base = ((rx + dx) % NX) * NY
         pieces = []
-        for j in range(NY):
-            even, odd_x = xall[0, base // 2 + j], xall[1, base // 2 + j]
+        for j in range(NY // 2):
+            even, odd_x = xall[base + 2 * j], xall[base + 2 * j + 1]
             pieces += [even[:, 0:128], jnp.where(low_half, even[:, 128:256], odd_x[:, 0:128]), odd_x[:, 128:256]]
             even_st = even_st + even[:, 128:256].astype(F32)
             odd_st = odd_st + odd_x[:, 0:128].astype(F32)
-        xs = jnp.concatenate(pieces, axis=1)
-        rows = pl.ds(pl.multiple_of(base * WIDTH, PER_X * WIDTH), PER_X * WIDTH)
-        inner_gate = inner_gate + dot(xs, wgu[0, rows, :])
-        inner_up = inner_up + dot(xs, wgu[1, rows, :])
+        rows = pl.ds(pl.multiple_of(base * WIDTH, NY * WIDTH), NY * WIDTH)
+        inner = inner + dot(jnp.concatenate(pieces, axis=1), wx[rows, :])
     st = pltpu.roll(even_st, 64, 1) + odd_st
+    stsend[...] = st
+    to_partner(9, stsend, strecv, 0)
+    insend[...] = inner.astype(BF16)
+    to_partner(8, insend, inrecv, 0)
+    pltpu.make_async_copy(strecv, strecv, recv_sem.at[RECV[9]]).wait()
+    st = st + strecv[...]
     st = st + pltpu.roll(st, 112, 1) + pltpu.roll(st, 96, 1)
     lane128 = iota((ROWS, 128), 1)
     squares = jnp.sum(jnp.where(lane128 == 8, st, 0.0), axis=1, keepdims=True)
@@ -489,21 +513,20 @@
     own_logit = jnp.sum(jnp.where(lane128 == c, logits, 0.0), axis=1, keepdims=True)
     other = jnp.sum(jnp.where((pair > 0.0) & (lane128 != c), logits, 0.0), axis=1, keepdims=True)
     share = 1.0 / (1.0 + jnp.exp(other - own_logit))
-    inner_gate = inner_gate * inverse
-    inner_up = inner_up * inverse
+    pltpu.make_async_copy(inrecv, inrecv, recv_sem.at[RECV[8]]).wait()
+    theirs = inrecv[...].astype(F32)
+    pair_of = [theirs[:, i * FSLICE : (i + 1) * FSLICE] for i in (1, 0, 3, 2)]
+    inner = (inner + jnp.concatenate(pair_of, axis=1)) * inverse
+    inner_gate, inner_up = inner[:, 0 : 2 * FSLICE], inner[:, 2 * FSLICE :]
     act = (inner_gate / (1.0 + jnp.exp(-inner_gate)) * inner_up * share).astype(BF16)
-    asend2[...] = act
-    to_partner(9, asend2, arecv2, 0)
-    half = wd.at[:, pl.ds(0, FSLICE)]
+    half = wd.at[pl.ds(0, FSLICE)]
     pltpu.make_async_copy(half, half, down_sem.at[0]).wait()
     pltpu.make_async_copy(half, half, down_sem.at[2]).wait()
-    pltpu.make_async_copy(arecv2, arecv2, recv_sem.at[RECV[9]]).wait()
-    other = arecv2[...]
-    act = jnp.concatenate([jnp.where(rc == 0, act, other), jnp.where(rc == 0, other, act)], axis=1)
     for dx in FAR_FIRST:
         base = ((rx + dx) % NX) * NY
+        y = dot(act, wd[:, pl.ds(pl.multiple_of(base * WPAD, NY * WPAD), NY * WPAD)])
         for j in range(NY):
-            ypair[base + j] = dot(act, wd[base + j]).astype(BF16)
+            ypair[base + j] = y[:, j * WPAD : (j + 1) * WPAD].astype(BF16)
         if dx == 0:
             yrec[chip] = ypair[chip]
         to_chips(6, lambda peer: ypair.at[peer], yrec.at[chip], dx)
@@ -536,8 +559,9 @@
     wait_for(send_sem.at[4], trec, NC - 1)
     wait_for(send_sem.at[5], yrec, CHIPS - 1)
     wait_for(send_sem.at[6], yrec, CHIPS - 1)
-    wait_for(send_sem.at[8], yrec, CHIPS)
-    pltpu.make_async_copy(arecv2, arecv2, send_sem.at[9]).wait()
+    pltpu.make_async_copy(inrecv, inrecv, send_sem.at[8]).wait()
+    pltpu.make_async_copy(strecv, strecv, send_sem.at[9]).wait()
+    pltpu.make_async_copy(half_x, half_x, down_sem.at[4]).wait()
     pltpu.make_async_copy(half, half, down_sem.at[1]).wait()
     wait_for(send_sem.at[7], zrec, NC - 1)
 
@@ -603,8 +627,8 @@
             pltpu.VMEM((2, 2, CTX, HD), BF16),
             pltpu.VMEM((2, SLOTS, PAGE, HD), BF16),
             pltpu.VMEM((WIDTH, GROUP * HD), BF16),
-            pltpu.VMEM((2, D, FSLICE), BF16),
-            pltpu.VMEM((CHIPS, NCORE * FSLICE, WPAD), BF16),
+            pltpu.VMEM((D // NCORE, 4 * FSLICE), BF16),
+            pltpu.VMEM((NCORE * FSLICE, CHIPS * WPAD), BF16),
             pltpu.VMEM((HROWS, HD), BF16),
             pltpu.VMEM((NR, HROWS, HD), BF16),
             pltpu.VMEM((NR, HROWS, HD), BF16),
@@ -614,9 +638,11 @@
             pltpu.VMEM((NC, ROWS, WPAD), BF16),
             pltpu.VMEM((NC, ROWS, WPAD), BF16),
             pltpu.VMEM((ROWS, WPAD), BF16),
-            pltpu.VMEM((NCORE, CHIPS, ROWS, WPAD), BF16),
-            pltpu.VMEM((ROWS, FSLICE), BF16),
-            pltpu.VMEM((ROWS, FSLICE), BF16),
+            pltpu.VMEM((CHIPS, ROWS, WPAD), BF16),
+            pltpu.VMEM((ROWS, 4 * FSLICE), BF16),
+            pltpu.VMEM((ROWS, 4 * FSLICE), BF16),
+            pltpu.VMEM((ROWS, 128), F32),
+            pltpu.VMEM((ROWS, 128), F32),
             pltpu.VMEM((CHIPS, ROWS, WPAD), BF16),
             pltpu.VMEM((CHIPS, ROWS, WPAD), BF16),
             pltpu.VMEM((NC, 2 * BLOCK, 128), BF16),
@@ -634,8 +660,8 @@
             pltpu.VMEM((SEQS, WPAD), F32),
             pltpu.VMEM((SEQS, GROUP * HD), BF16),
             pltpu.VMEM((BLOCK, WPAD), F32),
-            pltpu.SemaphoreType.DMA((14,)),
-            pltpu.SemaphoreType.DMA((3,)),
+            pltpu.SemaphoreType.DMA((13,)),
+            pltpu.SemaphoreType.DMA((6,)),
             pltpu.SemaphoreType.DMA((10,)),
             pltpu.SemaphoreType.DMA((25,)),
         ],

time: 51.2 us -> 51.4 us (level)
  Pallas kernels: 50 us -> 50.7 us
    pallas_call x1, Pallas kernels: 50 us -> 50.7 us  [body(): pl.pallas_call(kernel, out_shape=jax.ShapeDtypeStruct((BLOCK, WIDTH), BF1...]
where the time goes in v4:
time: 51.4 us; the launch traced here: 51.3 us
  Pallas kernels  50.7 us (99%)
  local copies, waits for them, and re-layouts  0.6 us (1%)
    pallas_call x1, Pallas kernels, body(): pl.pallas_call(kernel, out_shape=jax.ShapeDtypeStruct((BLOCK, WIDTH), BF1...  50.7 us

profile of v4, /device:TPU:1, one launch (start us, length us, event | category | flops | bytes accessed | tf_op | source)
XLA Modules:
  0.0 51.3 jit_solution(13886974113633312262)
XLA Ops:
  0.0 50.7 %layer.1 = bf16[8,192]{1,0:T(8,128)(2,1)S(1)} custom-call(s32[2]{0:T(128)} %lengths_h.1, s32[4,32]{1,0:T(4,128)} %bitcast.9, s32[2,8]{1,0:T(2,128)} %bitcast.10, bf16[8,192]{1,0:T(8,128)(2,1)} %hidden_h.1, bf16[2,768]{1,0:T(2,128)(2,1)} %queries_h.1, bf16[2,128]{1,0:T(2,128)(2,1)} %new_keys_h.1, bf16[2,128]{1,0:T(2,128)(2,1)} %new_values_h.1, ...), custom_call_target="tpu_custom_call" | custom-call | tf_op jit(solution)/shard_map/layer/pallas_call | solution.py:611
  50.7 0.6 %copy.20 = bf16[8,192]{1,0:T(8,128)(2,1)} copy(bf16[8,192]{1,0:T(8,128)(2,1)S(1)} %layer.1) | data formatting | bytes 6144
